TPU v7x, 8 devices: a whole 2x2x1 slice. The times are simulated.
8 devices in a mesh: dp: 2 (over z, y), tp: 4 (over x, core).
Axes of the slice: x: 2, y: 2, z: 1, core: 2. Of those that a mesh axis runs over, the one named last changes fastest.
Arguments:
- hidden: bfloat16 [6, 512, 896], P('dp')
- norm_w: bfloat16 [896], replicated
- embed_table: bfloat16 [151936, 896], P('tp')
- labels: int32 [6, 512], P('dp')
- loss_mask: int32 [6, 512], P('dp')
Outputs:
- output 1: float32 [], replicated
- output 2: bfloat16 [6, 512, 896], P('dp')
- output 3: float32 [896], replicated
- output 4: float32 [151936, 896], P('tp')
All inputs are finite; a program needn't handle non-finite values.
Results may differ from a plain program's by a relative error of at most 0.001.
Values sent between devices are 32-bit elements.
A program may use at most 1 GiB of HBM per device.

v0:
```python
import jax
import jax.numpy as jnp
from jax import lax
from jax.sharding import PartitionSpec as P

SOFT_CAP = 30.0


def norm_apply(hid_rows, gain32):
    h32 = hid_rows.astype(jnp.float32)
    inv_rms = lax.rsqrt(jnp.mean(h32 * h32, axis=-1, keepdims=True) + 1e-6)
    return h32 * inv_rms * (1.0 + gain32)


def solution(mesh):
    def local_step(hidden, norm_w, embed_table, labels, loss_mask):
        batch_rows, seq_len, model_dim = hidden.shape
        vocab_local = embed_table.shape[0]
        tokens = batch_rows * seq_len
        hid_rows = hidden.reshape(tokens, model_dim)
        mask_rows = loss_mask.reshape(tokens).astype(jnp.float32)
        tok_count = jnp.maximum(lax.psum(jnp.sum(mask_rows), 'dp'), 1.0)
        normed, norm_back = jax.vjp(norm_apply, hid_rows, norm_w.astype(jnp.float32))
        normed_bf = normed.astype(jnp.bfloat16)
        logits = jnp.einsum('td,vd->tv', normed_bf, embed_table, preferred_element_type=jnp.float32)
        capped = SOFT_CAP * jnp.tanh(logits / SOFT_CAP)
        row_max = lax.pmax(jnp.max(capped, axis=-1), 'tp')
        exp_shift = jnp.exp(capped - row_max[:, None])
        row_sum = lax.psum(jnp.sum(exp_shift, axis=-1), 'tp')
        local_ids = labels.reshape(tokens) - lax.axis_index('tp') * vocab_local
        onehot = lax.broadcasted_iota(jnp.int32, (1, vocab_local), 1) == local_ids[:, None]
        picked = lax.psum(jnp.sum(jnp.where(onehot, capped, 0.0), axis=-1), 'tp')
        tok_loss = jnp.log(row_sum) + row_max - picked
        mean_loss = lax.psum(jnp.sum(mask_rows * tok_loss), 'dp') / tok_count
        tok_scale = mask_rows / tok_count
        cap_ratio = capped / SOFT_CAP
        grad_logit = ((exp_shift / row_sum[:, None] - onehot.astype(jnp.float32)) * tok_scale[:, None] * (1.0 - cap_ratio * cap_ratio)).astype(jnp.bfloat16)
        grad_part = jnp.einsum('tv,vd->td', grad_logit, embed_table, preferred_element_type=jnp.float32)
        grad_x = lax.psum(grad_part, 'tp')
        grad_rows, grad_gain = norm_back(grad_x)
        grad_gain = lax.psum(grad_gain, 'dp')
        table_part = jnp.einsum('tv,td->vd', grad_logit, normed_bf, preferred_element_type=jnp.float32)
        grad_table = lax.psum(table_part, 'dp')
        return mean_loss, grad_rows.reshape(batch_rows, seq_len, model_dim), grad_gain, grad_table

    return jax.shard_map(local_step, mesh=mesh, in_specs=(P('dp', None, None), P(None), P('tp', None), P('dp', None), P('dp', None)), out_specs=(P(), P('dp', None, None), P(None), P('tp', None)), check_vma=False)
```

profile of v0, /device:TPU:0, one launch (start us, length us, event | category | flops | bytes accessed | tf_op | source)
XLA Modules:
  0.0 3697.9 jit_solution(6362644642017108104)
XLA Ops:
  7.2 1.3 convert_reduce_fusion
  8.5 0.7 convert_element_type.35
  9.2 6.9 psum.52
  16.1 0.7 convert_add_fusion
  16.8 0.7 broadcast_subtract_fusion
  17.5 0.6 sub.37
  18.1 0.6 convert_element_type.36
  18.7 2.4 fusion.8
  21.7 0.6 copy-done.3
  22.3 2.5 fusion.6
  24.8 142.2 %fusion.2 = (f32[1536]{0:T(1024)S(1)}, f32[1536,37984]{0,1:T(8,128)}) fusion(bf16[1536,896]{1,0:T(8,128)(2,1)S(1)} %fusion.6, bf16[37984,896]{1,0:T(8,128)(2,1)} %param.7), kind=kOutput, calls=%fused_computation.7 | convolution fusion | flops 104726446080 | bytes 304199680 | tf_op jit(solution)/shard_map/td,vd->tv/dot_general | solution.py:25
  167.0 5.9 pmax.7
  173.6 88.9 %fusion.1 = (f32[1536]{0:T(1024)S(1)}, f32[1536]{0:T(1024)S(1)}) fusion(f32[1536,37984]{0,1:T(8,128)} %get-tuple-element.15, f32[1536]{0:T(1024)S(1)} %pmax.7, s32[1536]{0:T(1024)S(1)} %copy-done.5), kind=kLoop, calls=%fused_computation.6 | loop fusion | flops 408400896 | bytes 233398272 | tf_op jit(solution)/shard_map/reduce_sum | solution.py:29
  262.5 11.4 all-reduce
  273.9 0.6 broadcast_divide_fusion
  274.5 123.8 %multiply_convert_fusion = bf16[1536,37984]{0,1:T(8,128)(2,1)} fusion(f32[1536,37984]{0,1:T(8,128)} %get-tuple-element.15, f32[1536]{0:T(1024)S(1)} %get-tuple-element.12, f32[1536]{0:T(1024)S(1)} %get-tuple-element.9, s32[1536]{0:T(1024)S(1)} %copy-done.5, f32[1536]{0:T(1024)S(1)} %pmax.7), kind=kLoop, calls=%fused_computation | loop fusion | flops 700121088 | bytes 350085120 | tf_op jit(solution)/shard_map/convert_element_type | solution.py:37
  398.4 133.3 %fusion.10 = f32[1536,896]{1,0:T(8,128)} fusion(bf16[1536,37984]{0,1:T(8,128)(2,1)} %multiply_convert_fusion, bf16[37984,896]{1,0:T(8,128)(2,1)} %param.7), kind=kOutput, calls=%fused_computation.27 | convolution fusion | flops 104551415808 | bytes 190259200 | tf_op jit(solution)/shard_map/tv,vd->td/dot_general | solution.py:38
  531.9 132.2 %fusion.11 = f32[37984,896]{1,0:T(8,128)} fusion(bf16[1536,37984]{0,1:T(8,128)(2,1)} %multiply_convert_fusion, bf16[1536,896]{1,0:T(8,128)(2,1)S(1)} %copy-done.2), kind=kOutput, calls=%fused_computation.28 | convolution fusion | flops 104551415808 | bytes 255574016 | tf_op jit(solution)/shard_map/tv,td->vd/dot_general | solution.py:42
  664.2 1.7 copy-done
  665.9 4.3 fusion.7
  670.1 5.9 all-reduce.1
  676.7 5.3 fusion.3
  682.0 2918.3 %all-reduce.7.cloned.1.call-done = f32[37984,896]{1,0:T(8,128)} async-done(((f32[37984,896]{1,0:T(8,128)}), f32[37984,896]{1,0:T(8,128)}) %all-reduce.7.cloned.1.call-update) | async-done | bytes 136134672 | tf_op jit(solution)/shard_map/psum | solution.py:43
  3600.3 89.2 %copy.11 = f32[37984,896]{1,0:T(8,128)} copy(f32[37984,896]{1,0:T(8,128)} %all-reduce.7.cloned.1.call-done) | data formatting | bytes 272269312
  (29 shorter events, 1.0 us)
Async XLA Ops:
  7.2 657.0 %all-reduce.5.cloned.1.call-start = ((), (), s32[]{:S(2)}) async-start(), calls=%async_computation | async-start | bytes 11010048 | tf_op jit(solution)/shard_map/psum | solution.py:39
  16.8 4.9 copy-start.8
  21.1 0.6 copy-start.6
  21.7 0.6 copy-start.3
  24.8 142.2 %copy-start.1 = (bf16[1536,896]{1,0:T(8,128)(2,1)}, bf16[1536,896]{1,0:T(8,128)(2,1)S(1)}, u32[]{:S(2)}) copy-start(bf16[1536,896]{1,0:T(8,128)(2,1)S(1)} %fusion.6) | copy-start | bytes 8257540
  24.8 148.8 %copy-start.5 = (s32[1536]{0:T(1024)S(1)}, s32[1536]{0:T(1024)}, u32[]{:S(2)}) copy-start(s32[1536]{0:T(1024)} %sub.37) | copy-start | bytes 18436
  173.6 100.3 %copy-start.10 = (f32[1536]{0:T(1024)S(1)}, f32[1536]{0:T(1024)}, u32[]{:S(2)}) copy-start(f32[1536]{0:T(1024)} %convert_element_type.36) | copy-start | bytes 18436
  398.4 133.6 %copy-start.2 = (bf16[1536,896]{1,0:T(8,128)(2,1)S(1)}, bf16[1536,896]{1,0:T(8,128)(2,1)}, u32[]{:S(2)}) copy-start(bf16[1536,896]{1,0:T(8,128)(2,1)} %copy-done.1) | copy-start | bytes 8257540
  531.7 3068.7 %all-reduce.7.cloned.1.call-start = ((), (), s32[]{:S(2)}) async-start(), calls=%async_computation.1 | async-start | bytes 272269312 | tf_op jit(solution)/shard_map/psum | solution.py:43
  664.1 1.8 copy-start
  664.1 1.8 copy-start.4
  664.1 1.8 copy-start.9
  664.1 12.6 copy-start.7
Sparse Core Ops, SparseCore 0:
  531.8 101.6 all-reduce.4
  664.2 2936.0 all-reduce.6
where the time goes:
time: 3710 us; the launch traced here: 3700 us
  waiting for transfers between devices  2920 us (79%)
  matrix products  408 us (11%)
  other arithmetic  231 us (6%)
  local copies, waits for them, and re-layouts  93.4 us (3%)
    psum x1, waiting for transfers between devices, local_step(): grad_table = lax.psum(table_part, 'dp')  2920 us
    dot_general x1, matrix products, local_step(): jnp.einsum('td,vd->tv', normed_bf, embed_table, preferred_element_type=jn...  142 us
    dot_general x1, matrix products, local_step(): jnp.einsum('tv,vd->td', grad_logit, embed_table, preferred_element_type=j...  133 us
    dot_general x1, matrix products, local_step(): jnp.einsum('tv,td->vd', grad_logit, normed_bf, preferred_element_type=jnp...  132 us
    convert_element_type x1, other arithmetic, local_step(): ((exp_shift / row_sum[:, None] - onehot.astype(jnp.float32)) * tok_scale[...  124 us
    unnamed x23, local copies, waits for them, and re-layouts  92.2 us
    reduce_sum x1, other arithmetic, local_step(): row_sum = lax.psum(jnp.sum(exp_shift, axis=-1), 'tp')  88.9 us
  transfers between devices with their start and end apart: 2, of which 1 were waited for; matrix products, arithmetic and copies ran while one was open for 4% of the time, Pallas kernels for 0%

commit v1 on v0

v1 whole, which is shorter than its diff:
```python
import functools
import jax
import jax.numpy as jnp
from jax import lax
from jax.experimental import pallas as pl
from jax.experimental.pallas import tpu as pltpu
from jax.sharding import PartitionSpec as P

SOFT_CAP = 30.0
LOG2E = 1.4426950408889634
CAP2 = SOFT_CAP * LOG2E
VMEM_LIMIT = 60 * 1024 * 1024


def norm_apply(hid_rows, gain32):
    h32 = hid_rows.astype(jnp.float32)
    inv_rms = lax.rsqrt(jnp.mean(h32 * h32, axis=-1, keepdims=True) + 1e-6)
    return h32 * inv_rms * (1.0 + gain32)


def chunks(total, size):
    return [(s, min(size, total - s)) for s in range(0, total, size)]


def per_block(nblk, rows, tail, body):
    if tail == 0:
        body(rows)
        return
    i = pl.program_id(0)

    @pl.when(i < nblk - 1)
    def _():
        body(rows)

    @pl.when(i == nblk - 1)
    def _():
        body(tail)


def row_hits(rows, cols, base, labels):
    ids = lax.broadcasted_iota(jnp.int32, (rows, cols), 0)
    return ids == (labels - base)


def logits_kernel(nblk, bv, tail, e_ref, xt_ref, lab_ref, t_ref, sum_ref, pick_ref):
    i = pl.program_id(0)

    @pl.when(i == 0)
    def _():
        sum_ref[...] = jnp.zeros_like(sum_ref)
        pick_ref[...] = jnp.zeros_like(pick_ref)

    tokens = xt_ref.shape[1]

    def body(rows):
        for m, mm in chunks(rows, 256):
            for n, nn in chunks(tokens, 512):
                cols = slice(n, n + nn)
                z = jnp.dot(e_ref[m:m + mm, :], xt_ref[:, cols], preferred_element_type=jnp.float32)
                t = jnp.tanh(z * (1.0 / SOFT_CAP))
                t_ref[m:m + mm, cols] = t
                e = jnp.exp2(t * CAP2)
                sum_ref[:, cols] += jnp.sum(e.reshape(mm // 8, 8, nn), axis=0)
                hit = row_hits(mm, nn, i * bv + m, lab_ref[:, cols])
                pick_ref[:, cols] += jnp.sum(jnp.where(hit, t, 0.0).reshape(mm // 8, 8, nn), axis=0)

    per_block(nblk, bv, tail, body)


def grad_of(t, base, lab, lz, ts):
    p = jnp.exp2(t * CAP2 - lz)
    hit = row_hits(t.shape[0], t.shape[1], base, lab)
    return (jnp.where(hit, p - 1.0, p) * ts * (1.0 - t * t)).astype(jnp.bfloat16)


def grad_x_kernel(nblk, bv, tail, e_ref, t_ref, lab_ref, lz_ref, ts_ref, gx_ref, et_ref, g_ref):
    i = pl.program_id(0)

    @pl.when(i == 0)
    def _():
        gx_ref[...] = jnp.zeros_like(gx_ref)

    tokens = t_ref.shape[1]

    def body(rows):
        for m, mm in chunks(rows, 256):
            et_ref[:, m:m + mm] = e_ref[m:m + mm, :].T
        for n, nn in chunks(tokens, 512):
            cols = slice(n, n + nn)
            for m, mm in chunks(rows, 64):
                g_ref[m:m + mm, cols] = grad_of(
                    t_ref[m:m + mm, cols], i * bv + m, lab_ref[:, cols], lz_ref[:, cols], ts_ref[:, cols])
            gx_ref[:, cols] += jnp.dot(et_ref[:, :rows], g_ref[:rows, cols], preferred_element_type=jnp.float32)

    per_block(nblk, bv, tail, body)


def grad_table_kernel(nblk, bv, tail, e_ref, t_ref, xto_ref, xs_ref, xo_ref, lab_ref, lz_ref, ts_ref, de_ref, g_ref, go_ref):
    i = pl.program_id(0)
    tokens = t_ref.shape[1]

    def body(rows):
        for n, nn in chunks(tokens, 512):
            cols = slice(n, n + nn)
            for m, mm in chunks(rows, 64):
                g_ref[m:m + mm, cols] = grad_of(
                    t_ref[m:m + mm, cols], i * bv + m, lab_ref[0:1, cols], lz_ref[0:1, cols], ts_ref[0:1, cols])
            for m, mm in chunks(rows, 256):
                z = jnp.dot(e_ref[m:m + mm, :], xto_ref[:, cols], preferred_element_type=jnp.float32)
                t = jnp.tanh(z * (1.0 / SOFT_CAP))
                go_ref[m:m + mm, cols] = grad_of(
                    t, i * bv + m, lab_ref[1:2, cols], lz_ref[1:2, cols], ts_ref[1:2, cols])
        part = jnp.dot(g_ref[:rows, :], xs_ref[...], preferred_element_type=jnp.float32)
        de_ref[:rows, :] = part + jnp.dot(go_ref[:rows, :], xo_ref[...], preferred_element_type=jnp.float32)

    per_block(nblk, bv, tail, body)


def prep_kernel(x32_ref, x_ref, xt_ref):
    x = x32_ref[...].astype(jnp.bfloat16)
    x_ref[...] = x
    xt_ref[...] = x.T


def whole(shape):
    return pl.BlockSpec(shape, lambda *_: (0,) * len(shape))


def params():
    return pltpu.CompilerParams(dimension_semantics=("arbitrary",), vmem_limit_bytes=VMEM_LIMIT)


def solution(mesh):
    n_dp = mesh.shape['dp']
    swap = [(i, n_dp - 1 - i) for i in range(n_dp)]

    def local_step(hidden, norm_w, embed_table, labels, loss_mask):
        batch_rows, seq_len, dim = hidden.shape
        vocab = embed_table.shape[0]
        tokens = batch_rows * seq_len
        hid_rows = hidden.reshape(tokens, dim)
        mask_own = loss_mask.reshape(1, tokens).astype(jnp.float32)
        normed, norm_back = jax.vjp(norm_apply, hid_rows, norm_w.astype(jnp.float32))
        x_own = normed.astype(jnp.bfloat16)
        other32 = lax.ppermute(normed, 'dp', swap)
        base = lax.axis_index('tp') * vocab
        lab_own = labels.reshape(1, tokens) - base
        lab_other = lax.ppermute(labels.reshape(1, tokens), 'dp', swap) - base

        bv = 1024
        nblk = pl.cdiv(vocab, bv)
        tail = vocab % bv
        row = whole((1, tokens))
        row2 = whole((2, tokens))
        e_spec = pl.BlockSpec((bv, dim), lambda i: (i, 0))
        t_spec = pl.BlockSpec((bv, tokens), lambda i: (i, 0))
        flops = 2 * tokens * vocab * dim
        t_own, sums, picks = pl.pallas_call(
            functools.partial(logits_kernel, nblk, bv, tail),
            grid=(nblk,),
            in_specs=[e_spec, whole((dim, tokens)), row],
            out_specs=[t_spec, whole((8, tokens)), whole((8, tokens))],
            out_shape=[jax.ShapeDtypeStruct((vocab, tokens), jnp.float32)]
            + [jax.ShapeDtypeStruct((8, tokens), jnp.float32)] * 2,
            compiler_params=params(),
            cost_estimate=pl.CostEstimate(flops=flops, bytes_accessed=vocab * (tokens * 4 + dim * 2), transcendentals=2 * vocab * tokens),
            name="logits",
        )(embed_table, x_own.T, lab_own)

        stat = jnp.stack([jnp.sum(sums, axis=0), jnp.sum(picks, axis=0)])
        stat = lax.psum(stat, 'tp')
        pack_own = jnp.concatenate([stat, mask_own], axis=0)
        pack_other = lax.ppermute(pack_own, 'dp', swap)
        z_both = jnp.stack([pack_own[0], pack_other[0]])
        pick_both = jnp.stack([pack_own[1], pack_other[1]]) * SOFT_CAP
        mask_both = jnp.stack([pack_own[2], pack_other[2]])
        tok_count = jnp.maximum(jnp.sum(mask_both), 1.0)
        mean_loss = jnp.sum(mask_both * (jnp.log(z_both) - pick_both)) / tok_count
        lz = jnp.log2(z_both)
        ts = mask_both / tok_count
        lab = jnp.concatenate([lab_own, lab_other], axis=0)

        gxt = pl.pallas_call(
            functools.partial(grad_x_kernel, nblk, bv, tail),
            grid=(nblk,),
            in_specs=[e_spec, t_spec, row, row, row],
            out_specs=whole((dim, tokens)),
            out_shape=jax.ShapeDtypeStruct((dim, tokens), jnp.float32),
            scratch_shapes=[pltpu.VMEM((dim, bv), jnp.bfloat16), pltpu.VMEM((bv, tokens), jnp.bfloat16)],
            compiler_params=params(),
            cost_estimate=pl.CostEstimate(flops=flops, bytes_accessed=vocab * (tokens * 4 + dim * 2), transcendentals=vocab * tokens),
            name="grad_x",
        )(embed_table, t_own, lab_own, lz[0:1], ts[0:1])
        grad_x = lax.psum(gxt, 'tp').T

        x_other, xt_other = pl.pallas_call(
            prep_kernel,
            out_shape=[jax.ShapeDtypeStruct((tokens, dim), jnp.bfloat16), jax.ShapeDtypeStruct((dim, tokens), jnp.bfloat16)],
            compiler_params=pltpu.CompilerParams(vmem_limit_bytes=VMEM_LIMIT),
            name="prep_other",
        )(other32)

        bt = 512
        nblk_t = pl.cdiv(vocab, bt)
        tail_t = vocab % bt
        grad_table = pl.pallas_call(
            functools.partial(grad_table_kernel, nblk_t, bt, tail_t),
            grid=(nblk_t,),
            in_specs=[
                pl.BlockSpec((bt, dim), lambda i: (i, 0)), pl.BlockSpec((bt, tokens), lambda i: (i, 0)),
                whole((dim, tokens)), whole((tokens, dim)), whole((tokens, dim)), row2, row2, row2],
            out_specs=pl.BlockSpec((bt, dim), lambda i: (i, 0)),
            out_shape=jax.ShapeDtypeStruct((vocab, dim), jnp.float32),
            scratch_shapes=[pltpu.VMEM((bt, tokens), jnp.bfloat16), pltpu.VMEM((bt, tokens), jnp.bfloat16)],
            compiler_params=params(),
            cost_estimate=pl.CostEstimate(flops=3 * flops, bytes_accessed=vocab * (tokens * 4 + dim * 6), transcendentals=3 * vocab * tokens),
            name="grad_table",
        )(embed_table, t_own, xt_other, x_own, x_other, lab, lz, ts)

        grad_rows, grad_gain = norm_back(grad_x)
        grad_gain = lax.psum(grad_gain, 'dp')
        return mean_loss, grad_rows.reshape(batch_rows, seq_len, dim), grad_gain, grad_table

    return jax.shard_map(local_step, mesh=mesh, in_specs=(P('dp', None, None), P(None), P('tp', None), P('dp', None), P('dp', None)), out_specs=(P(), P('dp', None, None), P(None), P('tp', None)), check_vma=False)
```

time: 3710 us -> 1010 us (0.27)
  waiting for transfers between devices: 2920 us -> 222 us
  Pallas kernels: 0 us -> 709 us
  matrix products: 408 us -> 0 us
  other arithmetic: 231 us -> 23.2 us
  local copies, waits for them, and re-layouts: 93.4 us -> 12.4 us
    psum x2 -> x1, waiting for transfers between devices: 2920 us -> 102 us  [local_step(): grad_x = lax.psum(gxt, 'tp').T]
    pallas_call x0 -> x4, Pallas kernels: none -> 709 us  [the longest x1 429 us: local_step(): pl.pallas_call(functools.partial(grad_table_kernel, nblk_t, bt, tail_t),...]
    dot_general x3 -> x0, matrix products: 408 us -> none  [the longest x1 142 us: local_step(): jnp.einsum('td,vd->tv', normed_bf, embed_table, preferred_element_type=jn...]
    convert_element_type x3 -> x1, other arithmetic: 127 us -> 2.48 us  [local_step(): x_own = normed.astype(jnp.bfloat16)]
    ppermute x0 -> x3, waiting for transfers between devices: none -> 120 us  [the longest x1 118 us: local_step(): lab_other = lax.ppermute(labels.reshape(1, tokens), 'dp', swap) - base]
    unnamed x23 -> x30, local copies, waits for them, and re-layouts: 92.2 us -> 1.94 us
    reduce_sum x2 -> x4, other arithmetic: 90.2 us -> 2.85 us  [the longest x2 1.63 us: local_step(): stat = jnp.stack([jnp.sum(sums, axis=0), jnp.sum(picks, axis=0)])]
  transfers between devices with their start and end apart: 2 -> 4, of which waited for: 1 -> 3; matrix products, arithmetic and copies ran while one was open for 4% -> 1% of each run, Pallas kernels for 0% -> 0%
where the time goes in v1:
time: 1010 us
  Pallas kernels  709 us (70%)
  waiting for transfers between devices  222 us (22%)
  other arithmetic  23.2 us (2%)
  blocking collectives  18.7 us (2%)
  between operations  17.3 us (2%)
  local copies, waits for them, and re-layouts  12.4 us (1%)
    pallas_call x1, Pallas kernels, local_step(): pl.pallas_call(functools.partial(grad_table_kernel, nblk_t, bt, tail_t),...  429 us
    pallas_call x1, Pallas kernels, local_step(): pl.pallas_call(functools.partial(logits_kernel, nblk, bv, tail), grid=(nb...  145 us
    pallas_call x1, Pallas kernels, local_step(): pl.pallas_call(functools.partial(grad_x_kernel, nblk, bv, tail), grid=(nb...  128 us
    ppermute x1, waiting for transfers between devices, local_step(): lab_other = lax.ppermute(labels.reshape(1, tokens), 'dp', swap) - base  118 us
    psum x1, waiting for transfers between devices, local_step(): grad_x = lax.psum(gxt, 'tp').T  102 us
  transfers between devices with their start and end apart: 4, of which 3 were waited for; matrix products, arithmetic and copies ran while one was open for 1% of the time, Pallas kernels for 0%

profile of v1, /device:TPU:0, one launch (start us, length us, event | category | flops | bytes accessed | tf_op | source)
XLA Modules:
  0.0 1005.6 jit_solution(83136745203954905)
XLA Ops:
  7.2 0.7 convert_add_fusion
  7.9 0.7 copy.12
  8.6 0.7 convert_bitcast_fusion
  9.3 2.4 fusion.4
  12.9 2.5 fusion.9.xs_ref
  15.4 3.1 copy.9.xt_ref
  19.1 145.4 %logits.1 = (f32[37984,1536]{1,0:T(8,128)}, f32[8,1536]{1,0:T(8,128)}, f32[8,1536]{1,0:T(8,128)}) custom-call(bf16[37984,896]{1,0:T(8,128)(2,1)} %e_ref.5, bf16[896,1536]{1,0:T(8,128)(2,1)} %copy.9.xt_ref, s32[1,1536]{1,0:T(1,128)} %broadcast_subtract_fusion.1.lab_ref), custom_call_target="tpu_custom_call" | custom-call | flops 104551415808 | bytes 301441024 | tf_op jit(solution)/shard_map/logits/pallas_call | solution.py:158
  164.6 0.8 reduce_sum.80
  165.4 0.8 reduce_sum.81
  166.3 13.0 %psum.21 = f32[2,1536]{1,0:T(2,128)S(1)} all-reduce(f32[2,1536]{1,0:T(2,128)S(1)} %pad_maximum_fusion.1), channel_id=1, replica_groups=mesh['dp'=2,'tp'=4] {'tp'}, use_global_device_ids=true, to_apply=%region_3.0 | all-reduce | flops 3072 | bytes 24576 | tf_op jit(solution)/shard_map/psum | solution.py:171
  179.3 1.5 collective-permute-start
  181.4 1.7 collective-permute-done
  183.1 0.6 slice_reduce_fusion
  185.0 0.6 broadcast_divide_fusion
  186.9 128.4 %grad_x.1 = f32[896,1536]{1,0:T(8,128)} custom-call(bf16[37984,896]{1,0:T(8,128)(2,1)} %e_ref.5, f32[37984,1536]{1,0:T(8,128)} %get-tuple-element.11.t_ref, s32[1,1536]{1,0:T(1,128)} %broadcast_subtract_fusion.1.lab_ref, f32[1,1536]{1,0:T(1,128)} %slice.33.lz_ref, f32[1,1536]{1,0:T(1,128)} %slice.34.ts_ref), custom_call_target="tpu_custom_call" | custom-call | flops 104551415808 | bytes 301441024 | tf_op jit(solution)/shard_map/grad_x/pallas_call | solution.py:183
  315.3 6.1 copy.10
  321.5 101.5 %all-reduce.2.cloned.1.call-done = f32[1536,896]{1,0:T(8,128)} async-done(((f32[1536,896]{1,0:T(8,128)}), f32[1536,896]{1,0:T(8,128)}) %all-reduce.2.cloned.1.call-update) | async-done | bytes 5505040 | tf_op jit(solution)/shard_map/psum | solution.py:194
  423.0 6.9 fusion.3
  429.8 1.5 collective-permute-start.1
  431.9 118.4 %collective-permute-done.2 = s32[1,1536]{1,0:T(1,128)S(1)} collective-permute-done((s32[1,1536]{1,0:T(1,128)S(1)}, s32[1,1536]{1,0:T(1,128)S(1)}, u32[]{:S(2)}, u32[]{:S(2)}) %collective-permute-start.2) | collective-permute-done | bytes 6176 | tf_op jit(solution)/shard_map/ppermute | solution.py:148
  551.5 5.7 psum.23
  557.3 5.3 fusion
  562.6 5.6 prep_other.1
  568.2 429.3 %grad_table.1 = f32[37984,896]{1,0:T(8,128)} custom-call(bf16[37984,896]{1,0:T(8,128)(2,1)} %e_ref.5, f32[37984,1536]{1,0:T(8,128)} %get-tuple-element.11.t_ref, bf16[896,1536]{1,0:T(8,128)(2,1)} %get-tuple-element.12.xto_ref, bf16[1536,896]{1,0:T(8,128)(2,1)} %copy-done.1, bf16[1536,896]{1,0:T(8,128)(2,1)} %get-tuple-element.13.xo_ref, ...), custom_call_target="tpu_custom_call" | custom-call | flops 313654247424 | bytes 437575680 | tf_op jit(solution)/shard_map/grad_table/pallas_call | solution.py:206
  (48 shorter events, 5.0 us)
Async XLA Ops:
  7.2 415.8 %all-reduce.2.cloned.1.call-start = ((), (), s32[]{:S(2)}) async-start(), calls=%async_computation | async-start | bytes 11010048 | tf_op jit(solution)/shard_map/psum | solution.py:194
  7.9 10.6 %copy-start.6 = (f32[896]{0:T(1024)}, f32[896]{0:T(1024)S(1)}, u32[]{:S(2)}) copy-start(f32[896]{0:T(1024)S(1)} %convert_add_fusion) | copy-start | bytes 10756
  8.6 9.9 copy-start.11
  11.7 0.6 copy-start.4
  12.3 0.6 copy-start.2
  15.4 149.1 %copy-start.1 = (bf16[1536,896]{1,0:T(8,128)(2,1)}, bf16[1536,896]{1,0:T(8,128)(2,1)S(1)}, u32[]{:S(2)}) copy-start(bf16[1536,896]{1,0:T(8,128)(2,1)S(1)} %fusion.9.xs_ref) | copy-start | bytes 8257540
  19.1 161.7 %copy-start.8 = (s32[3,512]{1,0:T(4,128)S(1)}, s32[3,512]{1,0:T(4,128)}, u32[]{:S(2)}) copy-start(s32[3,512]{1,0:T(4,128)} %param.9) | copy-start | bytes 18436
  179.3 3.8 collective-permute-start
  185.7 129.6 %copy-start.9 = (f32[2,1536]{1,0:T(2,128)}, f32[2,1536]{1,0:T(2,128)S(1)}, u32[]{:S(2)}) copy-start(f32[2,1536]{1,0:T(2,128)S(1)} %get-tuple-element.21.ts_ref) | copy-start | bytes 36868
  185.7 129.6 %copy-start.10 = (f32[2,1536]{1,0:T(2,128)}, f32[2,1536]{1,0:T(2,128)S(1)}, u32[]{:S(2)}) copy-start(f32[2,1536]{1,0:T(2,128)S(1)} %get-tuple-element.23.lz_ref) | copy-start | bytes 36868
  321.4 101.6 %copy-start = (bf16[3,512,896]{2,1,0:T(8,128)(2,1)S(1)}, bf16[3,512,896]{2,1,0:T(8,128)(2,1)}, u32[]{:S(2)}) copy-start(bf16[3,512,896]{2,1,0:T(8,128)(2,1)} %param.5) | copy-start | bytes 8257540
  321.4 101.6 %copy-start.3 = (f32[1536]{0:T(1024)S(1)}, f32[1536]{0:T(1024)}, u32[]{:S(2)}) copy-start(f32[1536]{0:T(1024)} %copy-done.2) | copy-start | bytes 18436
  321.4 101.6 %copy-start.7 = (f32[896]{0:T(1024)S(1)}, f32[896]{0:T(1024)}, u32[]{:S(2)}) copy-start(f32[896]{0:T(1024)} %copy-done.6) | copy-start | bytes 10756
  321.4 109.9 %copy-start.12 = (s32[1,1,3,512]{3,1,2,0:T(1,128)S(1)}, s32[1,1,3,512]{3,1,2,0:T(1,128)}, u32[]{:S(2)}) copy-start(s32[1,1,3,512]{3,1,2,0:T(1,128)} %copy-done.11) | copy-start | bytes 18436
  321.4 228.8 %copy-start.13 = (s32[1,1536]{1,0:T(1,128)S(1)}, s32[1,1536]{1,0:T(1,128)}, u32[]{:S(2)}) copy-start(s32[1,1536]{1,0:T(1,128)} %broadcast_subtract_fusion.1.lab_ref) | copy-start | bytes 18436
  321.4 235.8 %copy-start.5 = (f32[1536]{0:T(1024)S(1)}, f32[1536]{0:T(1024)}, u32[]{:S(2)}) copy-start(f32[1536]{0:T(1024)} %copy-done.4) | copy-start | bytes 18436
  429.8 132.8 %collective-permute-start.1 = (f32[1536,896]{1,0:T(8,128)}, f32[1536,896]{1,0:T(8,128)}, u32[]{:S(2)}, u32[]{:S(2)}) collective-permute-start(f32[1536,896]{1,0:T(8,128)} %get-tuple-element.16), channel_id=1, source_target_pairs={{0,4},{4,0},{1,5},{5,1},{2,6},{6,2},{3,7},{7,3}} | collective-permute-start | bytes 16515080 | tf_op jit(solution)/shard_map/ppermute | solution.py:145
  431.3 119.0 %collective-permute-start.2 = (s32[1,1536]{1,0:T(1,128)S(1)}, s32[1,1536]{1,0:T(1,128)S(1)}, u32[]{:S(2)}, u32[]{:S(2)}) collective-permute-start(s32[1,1536]{1,0:T(1,128)S(1)} %bitcast.32), channel_id=1, source_target_pairs={{0,4},{4,0},{1,5},{5,1},{2,6},{6,2},{3,7},{7,3}} | collective-permute-start | bytes 18440 | tf_op jit(solution)/shard_map/ppermute | solution.py:148
Sparse Core Ops, SparseCore 0:
  321.5 101.3 all-reduce.1

commit v2 on v0

v2 whole, which is shorter than its diff:
```python
import functools
import jax
import jax.numpy as jnp
from jax import lax
from jax.experimental import pallas as pl
from jax.experimental.pallas import tpu as pltpu
from jax.sharding import PartitionSpec as P

SOFT_CAP = 30.0
LOG2E = 1.4426950408889634
CAP2 = SOFT_CAP * LOG2E
VMEM_LIMIT = 60 * 1024 * 1024
TILE = 256


def norm_apply(hid_rows, gain32):
    h32 = hid_rows.astype(jnp.float32)
    inv_rms = lax.rsqrt(jnp.mean(h32 * h32, axis=-1, keepdims=True) + 1e-6)
    return h32 * inv_rms * (1.0 + gain32)


def chunks(total, size):
    return [(s, min(size, total - s)) for s in range(0, total, size)]


def per_width(n_tiles, tokens, body):
    full = tokens // TILE
    widths = list(range(max(1, full - 2), full + 1))
    for k, w in enumerate(widths):
        if len(widths) == 1:
            cond = True
        elif k == 0:
            cond = n_tiles <= w
        elif k == len(widths) - 1:
            cond = n_tiles >= w
        else:
            cond = n_tiles == w

        @pl.when(cond)
        def _():
            body(w * TILE)


def row_hits(rows, cols, base, labels):
    ids = lax.broadcasted_iota(jnp.int32, (rows, cols), 0)
    return ids == (labels - base)


def prep_kernel(hid_ref, mask_ref, dig_ref, gain_ref, hc_ref, x_ref, xt_ref, x32_ref, perm_ref, lab_ref):
    tokens = hid_ref.shape[0]
    mask = mask_ref[...]
    src = lax.broadcasted_iota(jnp.int32, (tokens, tokens), 0)
    dst = lax.broadcasted_iota(jnp.int32, (tokens, tokens), 1)
    upto = jnp.where(src <= dst, 1.0, 0.0).astype(jnp.bfloat16)
    count = jnp.dot(jnp.broadcast_to(mask, (8, tokens)).astype(jnp.bfloat16), upto, preferred_element_type=jnp.float32)
    place = jnp.where(mask > 0.0, count[0:1, :] - 1.0, -1.0).astype(jnp.int32)
    perm_ref[...] = jnp.where(src == place, 1.0, 0.0).astype(jnp.bfloat16)
    hc_ref[...] = jnp.dot(perm_ref[...], hid_ref[...], preferred_element_type=jnp.float32).astype(jnp.bfloat16)
    digits = lax.dot_general(dig_ref[...], perm_ref[...], (((1,), (1,)), ((), ())), preferred_element_type=jnp.float32)
    lab_ref[...] = digits[0:1, :] + 64.0 * digits[1:2, :] + 4096.0 * digits[2:3, :]
    for m, mm in chunks(tokens, TILE):
        rows = slice(m, m + mm)
        x32 = norm_apply(hc_ref[rows, :], gain_ref[...])
        x = x32.astype(jnp.bfloat16)
        x32_ref[rows, :] = x32
        x_ref[rows, :] = x
        xt_ref[:, rows] = x.T


def other_kernel(x32_ref, x_ref, xt_ref):
    x = x32_ref[...].astype(jnp.bfloat16)
    x_ref[...] = x
    xt_ref[...] = x.T


def logits_kernel(nblk, bv, tail, nt_ref, e_ref, xt_ref, lab_ref, t_ref, sum_ref, pick_ref):
    i = pl.program_id(0)
    tokens = xt_ref.shape[1]

    @pl.when(i == 0)
    def _():
        sum_ref[...] = jnp.zeros_like(sum_ref)
        pick_ref[...] = jnp.zeros_like(pick_ref)

    def body(rows, width):
        for m, mm in chunks(rows, 256):
            for n, nn in chunks(width, 512):
                cols = slice(n, n + nn)
                z = jnp.dot(e_ref[m:m + mm, :], xt_ref[:, cols], preferred_element_type=jnp.float32)
                t = jnp.tanh(z * (1.0 / SOFT_CAP))
                t_ref[m:m + mm, cols] = t
                e = jnp.exp2(t * CAP2)
                sum_ref[:, cols] += jnp.sum(e.reshape(mm // 8, 8, nn), axis=0)
                hit = row_hits(mm, nn, i * bv + m, lab_ref[:, cols])
                pick_ref[:, cols] += jnp.sum(jnp.where(hit, t, 0.0).reshape(mm // 8, 8, nn), axis=0)

    @pl.when(i < nblk - 1)
    def _():
        per_width(nt_ref[0], tokens, functools.partial(body, bv))

    @pl.when(i == nblk - 1)
    def _():
        body(tail, tokens)


def grad_of(t, base, lab, lz, ts):
    p = jnp.exp2(t * CAP2 - lz)
    hit = row_hits(t.shape[0], t.shape[1], base, lab)
    return (jnp.where(hit, p - 1.0, p) * ts * (1.0 - t * t)).astype(jnp.bfloat16)


def grad_x_kernel(nblk, bv, tail, nt_ref, e_ref, t_ref, lab_ref, lz_ref, ts_ref, gx_ref, et_ref, g_ref):
    i = pl.program_id(0)
    tokens = t_ref.shape[1]

    @pl.when(i == 0)
    def _():
        gx_ref[...] = jnp.zeros_like(gx_ref)

    def body(rows, width):
        for m, mm in chunks(rows, 256):
            et_ref[:, m:m + mm] = e_ref[m:m + mm, :].T
        for n, nn in chunks(width, 512):
            cols = slice(n, n + nn)
            for m, mm in chunks(rows, 64):
                g_ref[m:m + mm, cols] = grad_of(
                    t_ref[m:m + mm, cols], i * bv + m, lab_ref[:, cols], lz_ref[:, cols], ts_ref[:, cols])
            gx_ref[:, cols] += jnp.dot(et_ref[:, :rows], g_ref[:rows, cols], preferred_element_type=jnp.float32)

    @pl.when(i < nblk - 1)
    def _():
        per_width(nt_ref[0], tokens, functools.partial(body, bv))

    @pl.when(i == nblk - 1)
    def _():
        body(tail, tokens)


def grad_table_kernel(nblk, bv, tail, nt_ref, e_ref, t_ref, xto_ref, xs_ref, xo_ref, lab_ref, lz_ref, ts_ref, de_ref, g_ref):
    i = pl.program_id(0)
    tokens = t_ref.shape[1]

    def own(rows, width):
        for n, nn in chunks(width, 512):
            cols = slice(n, n + nn)
            for m, mm in chunks(rows, 64):
                g_ref[m:m + mm, cols] = grad_of(
                    t_ref[m:m + mm, cols], i * bv + m, lab_ref[0:1, cols], lz_ref[0:1, cols], ts_ref[0:1, cols])
        de_ref[:rows, :] = jnp.dot(g_ref[:rows, :width], xs_ref[:width, :], preferred_element_type=jnp.float32)

    def other(rows, width):
        for n, nn in chunks(width, 512):
            cols = slice(n, n + nn)
            for m, mm in chunks(rows, 256):
                z = jnp.dot(e_ref[m:m + mm, :], xto_ref[:, cols], preferred_element_type=jnp.float32)
                t = jnp.tanh(z * (1.0 / SOFT_CAP))
                g_ref[m:m + mm, cols] = grad_of(
                    t, i * bv + m, lab_ref[1:2, cols], lz_ref[1:2, cols], ts_ref[1:2, cols])
        de_ref[:rows, :] += jnp.dot(g_ref[:rows, :width], xo_ref[:width, :], preferred_element_type=jnp.float32)

    @pl.when(i < nblk - 1)
    def _():
        per_width(nt_ref[0], tokens, functools.partial(own, bv))
        per_width(nt_ref[1], tokens, functools.partial(other, bv))

    @pl.when(i == nblk - 1)
    def _():
        own(tail, tokens)
        other(tail, tokens)


def whole(shape):
    return pl.BlockSpec(shape, lambda *_: (0,) * len(shape))


def blocks(rows, cols):
    return pl.BlockSpec((rows, cols), lambda i, *_: (i, 0))


def params(**kw):
    return pltpu.CompilerParams(vmem_limit_bytes=VMEM_LIMIT, **kw)


def table_call(kernel, vocab, rows, in_specs, out_specs, out_shape, scratch, cost):
    nblk = pl.cdiv(vocab, rows)
    tail = vocab - (nblk - 1) * rows
    return pl.pallas_call(
        functools.partial(kernel, nblk, rows, tail),
        grid_spec=pltpu.PrefetchScalarGridSpec(
            num_scalar_prefetch=1, grid=(nblk,), in_specs=in_specs, out_specs=out_specs, scratch_shapes=scratch),
        out_shape=out_shape,
        compiler_params=params(dimension_semantics=("arbitrary",)),
        cost_estimate=cost,
    )


def solution(mesh):
    n_dp = mesh.shape['dp']
    swap = [(i, n_dp - 1 - i) for i in range(n_dp)]

    def local_step(hidden, norm_w, embed_table, labels, loss_mask):
        batch_rows, seq_len, dim = hidden.shape
        vocab = embed_table.shape[0]
        tokens = batch_rows * seq_len
        hid_rows = hidden.reshape(tokens, dim)
        mask_rows = loss_mask.reshape(1, tokens).astype(jnp.float32)
        gain = norm_w.astype(jnp.float32)
        lab_rows = labels.reshape(tokens)
        digits = jnp.stack([lab_rows & 63, (lab_rows >> 6) & 63, lab_rows >> 12] + [jnp.zeros_like(lab_rows)] * 5)
        f32, b16 = jnp.float32, jnp.bfloat16
        shape = jax.ShapeDtypeStruct
        hid_c, x_own, xt_own, x32, perm, lab_c = pl.pallas_call(
            prep_kernel,
            out_shape=[shape((tokens, dim), b16), shape((tokens, dim), b16), shape((dim, tokens), b16),
                       shape((tokens, dim), f32), shape((tokens, tokens), b16), shape((1, tokens), f32)],
            compiler_params=params(),
            name="prep",
        )(hid_rows, mask_rows, digits.astype(b16), gain.reshape(1, dim))
        other32 = lax.ppermute(x32, 'dp', swap)
        count = jnp.sum(mask_rows)
        mask_c = (jnp.arange(tokens, dtype=jnp.int32)[None, :] < count.astype(jnp.int32)).astype(f32)
        base = lax.axis_index('tp') * vocab
        lab_own = lab_c.astype(jnp.int32) - base
        nt_own = pl.cdiv(count.astype(jnp.int32), TILE).reshape(1)

        row = whole((1, tokens))
        row2 = whole((2, tokens))
        flops = 2 * tokens * vocab * dim
        elems = vocab * tokens

        bv = 2048
        t_own, sums, picks = table_call(
            logits_kernel, vocab, bv,
            [blocks(bv, dim), whole((dim, tokens)), row],
            [blocks(bv, tokens), whole((8, tokens)), whole((8, tokens))],
            [shape((vocab, tokens), f32), shape((8, tokens), f32), shape((8, tokens), f32)], [],
            pl.CostEstimate(flops=flops, bytes_accessed=elems * 4 + vocab * dim * 2, transcendentals=2 * elems),
        )(nt_own, embed_table, xt_own, lab_own)

        stat = lax.psum(jnp.stack([jnp.sum(sums, axis=0), jnp.sum(picks, axis=0)]), 'tp')
        pack_own = jnp.concatenate([stat, mask_c, lab_c], axis=0)
        pack_other = lax.ppermute(pack_own, 'dp', swap)
        z_both, pick_both, mask_both, lab_both = [jnp.stack([pack_own[k], pack_other[k]]) for k in range(4)]
        live = mask_both > 0.0
        z_both = jnp.where(live, z_both, 1.0)
        tok_count = jnp.maximum(jnp.sum(mask_both), 1.0)
        mean_loss = jnp.sum(jnp.where(live, jnp.log(z_both) - SOFT_CAP * pick_both, 0.0)) / tok_count
        lz = jnp.log2(z_both)
        ts = mask_both / tok_count
        lab = lab_both.astype(jnp.int32) - base
        nt_both = pl.cdiv(jnp.sum(mask_both, axis=1).astype(jnp.int32), TILE)

        bx = 1024
        gxt = table_call(
            grad_x_kernel, vocab, bx,
            [blocks(bx, dim), blocks(bx, tokens), row, row, row], whole((dim, tokens)), shape((dim, tokens), f32),
            [pltpu.VMEM((dim, bx), b16), pltpu.VMEM((bx, tokens), b16)],
            pl.CostEstimate(flops=flops, bytes_accessed=elems * 4 + vocab * dim * 2, transcendentals=elems),
        )(nt_own, embed_table, t_own, lab_own, lz[0:1], ts[0:1])
        grad_xt = lax.psum(gxt, 'tp')

        x_other, xt_other = pl.pallas_call(
            other_kernel, out_shape=[shape((tokens, dim), b16), shape((dim, tokens), b16)],
            compiler_params=params(), name="prep_other",
        )(other32)

        ts_late, _ = lax.optimization_barrier((ts, gxt[0, 0]))
        bt = 1024
        grad_table = table_call(
            grad_table_kernel, vocab, bt,
            [blocks(bt, dim), blocks(bt, tokens), whole((dim, tokens)), whole((tokens, dim)), whole((tokens, dim)),
             row2, row2, row2],
            blocks(bt, dim), shape((vocab, dim), f32), [pltpu.VMEM((bt, tokens), b16)],
            pl.CostEstimate(flops=3 * flops, bytes_accessed=elems * 4 + vocab * dim * 6, transcendentals=3 * elems),
        )(nt_both, embed_table, t_own, xt_other, x_own, x_other, lab, lz, ts_late)

        _, norm_back = jax.vjp(norm_apply, hid_c, gain)
        grad_rows, grad_gain = norm_back(grad_xt.T)
        grad_rows = jnp.einsum('it,id->td', perm, grad_rows, preferred_element_type=f32).astype(b16)
        grad_gain = lax.psum(grad_gain, 'dp')
        return mean_loss, grad_rows.reshape(batch_rows, seq_len, dim), grad_gain, grad_table

    return jax.shard_map(local_step, mesh=mesh, in_specs=(P('dp', None, None), P(None), P('tp', None), P('dp', None), P('dp', None)), out_specs=(P(), P('dp', None, None), P(None), P('tp', None)), check_vma=False)
```

time: 3710 us -> 896 us (0.24)
  waiting for transfers between devices: 2920 us -> 103 us
  Pallas kernels: 0 us -> 695 us
  matrix products: 408 us -> 10.3 us
  other arithmetic: 231 us -> 13.7 us
  local copies, waits for them, and re-layouts: 93.4 us -> 7.6 us
    psum x2 -> x1, waiting for transfers between devices: 2920 us -> 102 us  [local_step(): grad_xt = lax.psum(gxt, 'tp')]
    pallas_call x0 -> x5, Pallas kernels: none -> 695 us  [the longest x1 433 us: local_step(): table_call(grad_table_kernel, vocab, bt, [blocks(bt, dim), blocks(bt, tok...]
    dot_general x3 -> x1, matrix products: 408 us -> 10.3 us  [local_step(): jnp.einsum('it,id->td', perm, grad_rows, preferred_element_type=f32)]
    convert_element_type x4 -> x1, other arithmetic: 132 us -> 0.01 us  [local_step(): (jnp.arange(tokens, dtype=jnp.int32)[None, :] < count.astype(jnp.int32))....]
    unnamed x23 -> x12, local copies, waits for them, and re-layouts: 92.2 us -> 0.64 us
    reduce_sum x2 -> x5, other arithmetic: 90.2 us -> 4.3 us  [the longest x1 1.31 us: local_step(): count = jnp.sum(mask_rows)]
  transfers between devices with their start and end apart: 2 -> 3, of which waited for: 1 -> 2; matrix products, arithmetic and copies ran while one was open for 4% -> 3% of each run, Pallas kernels for 0% -> 14%
where the time goes in v2:
time: 896 us; the launch traced here: 889 us
  Pallas kernels  695 us (78%)
  waiting for transfers between devices  103 us (11%)
  starting transfers between devices  22.2 us (2%)
  blocking collectives  18.5 us (2%)
  between operations  18.1 us (2%)
  other arithmetic  13.7 us (2%)
  matrix products  10.3 us (1%)
    pallas_call x1, Pallas kernels, local_step(): table_call(grad_table_kernel, vocab, bt, [blocks(bt, dim), blocks(bt, tok...  433 us
    pallas_call x1, Pallas kernels, local_step(): table_call(grad_x_kernel, vocab, bx, [blocks(bx, dim), blocks(bx, tokens)...  122 us
    pallas_call x1, Pallas kernels, local_step(): table_call(logits_kernel, vocab, bv, [blocks(bv, dim), whole((dim, tokens...  119 us
    psum x1, waiting for transfers between devices, local_step(): grad_xt = lax.psum(gxt, 'tp')  102 us
    ppermute x1, starting transfers between devices, local_step(): pack_other = lax.ppermute(pack_own, 'dp', swap)  22.1 us
  transfers between devices with their start and end apart: 3, of which 2 were waited for; matrix products, arithmetic and copies ran while one was open for 3% of the time, Pallas kernels for 14%

profile of v2, /device:TPU:0, one launch (start us, length us, event | category | flops | bytes accessed | tf_op | source)
XLA Modules:
  0.0 888.7 jit_solution(3715641104848833615)
XLA Ops:
  7.2 0.7 convert_bitcast_fusion
  7.9 1.3 convert_reduce_fusion
  9.8 0.7 fusion.17
  10.6 1.3 reshape.113.gain_ref
  12.5 0.7 stack.32.dig_ref
  13.2 15.2 %prep.1 = (bf16[1536,896]{1,0:T(8,128)(2,1)}, bf16[1536,896]{1,0:T(8,128)(2,1)}, bf16[896,1536]{1,0:T(8,128)(2,1)}, f32[1536,896]{1,0:T(8,128)}, bf16[1536,1536]{1,0:T(8,128)(2,1)}, /*index=5*/f32[1,1536]{1,0:T(1,128)}) custom-call(bf16[1536,896]{1,0:T(8,128)(2,1)} %bitcast.22, f32[1,1536]{1,0:T(1,128)} %bitcast.26, bf16[8,1536]{1,0:T(8,128)(2,1)} %stack.32.dig_ref, ...), custom_call_target="tpu_custom_call" | custom-call | tf_op jit(solution)/shard_map/prep/pallas_call | solution.py:212
  28.4 1.3 convert_subtract_fusion.lab_ref
  29.6 119.4 %shard_map.84 = (f32[37984,1536]{1,0:T(8,128)}, f32[8,1536]{1,0:T(8,128)}, f32[8,1536]{1,0:T(8,128)}) custom-call(s32[1]{0:T(128)} %bitcast.nt_ref, bf16[37984,896]{1,0:T(8,128)(2,1)} %e_ref.5, bf16[896,1536]{1,0:T(8,128)(2,1)} %get-tuple-element.15.xt_ref, s32[1,1536]{1,0:T(1,128)} %convert_subtract_fusion.lab_ref), custom_call_target="tpu_custom_call" | custom-call | flops 104551415808 | bytes 301441024 | tf_op jit(solution)/shard_map/pallas_call | solution.py:232
  149.0 0.8 reduce_sum.99
  149.9 0.8 reduce_sum.98
  150.7 13.0 %psum.21 = f32[2,1536]{1,0:T(2,128)S(1)} all-reduce(f32[2,1536]{1,0:T(2,128)S(1)} %pad_maximum_fusion.1), channel_id=1, replica_groups=mesh['dp'=2,'tp'=4] {'tp'}, use_global_device_ids=true, to_apply=%region_3.0 | all-reduce | flops 3072 | bytes 24576 | tf_op jit(solution)/shard_map/psum | solution.py:240
  163.7 22.1 %collective-permute-start = (f32[4,1536]{1,0:T(4,128)S(1)}, f32[4,1536]{1,0:T(4,128)S(1)}, u32[]{:S(2)}, u32[]{:S(2)}) collective-permute-start(f32[4,1536]{1,0:T(4,128)S(1)} %pad_maximum_fusion), channel_id=1, source_target_pairs={{0,4},{4,0},{1,5},{5,1},{2,6},{6,2},{3,7},{7,3}} | collective-permute-start | bytes 73736 | tf_op jit(solution)/shard_map/ppermute | solution.py:242
  185.9 0.7 fusion.19
  186.6 1.3 collective-permute-done
  188.0 0.6 fusion.21
  189.8 0.7 fusion.20
  191.7 122.2 %shard_map.85 = f32[896,1536]{1,0:T(8,128)} custom-call(s32[1]{0:T(128)} %bitcast.nt_ref, bf16[37984,896]{1,0:T(8,128)(2,1)} %e_ref.5, f32[37984,1536]{1,0:T(8,128)} %get-tuple-element.20.t_ref, s32[1,1536]{1,0:T(1,128)} %convert_subtract_fusion.lab_ref, f32[1,1536]{1,0:T(1,128)} %slice.38.lz_ref, f32[1,1536]{1,0:T(1,128)} %slice.39.ts_ref), custom_call_target="tpu_custom_call" | custom-call | flops 104551415808 | bytes 301441024 | tf_op jit(solution)/shard_map/pallas_call | solution.py:254
  314.0 3.8 copy.9
  320.3 101.9 %all-reduce.2.cloned.1.call-done = f32[1536,896]{0,1:T(8,128)} async-done(((f32[1536,896]{0,1:T(8,128)}), f32[1536,896]{0,1:T(8,128)}) %all-reduce.2.cloned.1.call-update) | async-done | bytes 5505040 | tf_op jit(solution)/shard_map/psum | solution.py:260
  422.2 4.2 fusion.4
  426.4 5.5 psum.23
  432.0 10.3 %convolution_convert_fusion = bf16[1536,896]{1,0:T(8,128)(2,1)} fusion(bf16[1536,1536]{1,0:T(8,128)(2,1)} %get-tuple-element.19, bf16[1536,896]{0,1:T(8,128)(2,1)S(1)} %copy.9, f32[1536,896]{0,1:T(8,128)} %all-reduce.2.cloned.1.call-done, f32[1536]{0:T(1024)S(1)} %multiply_multiply_fusion, f32[1536]{0:T(1024)S(1)} %fusion.14, f32[896]{0:T(1024)S(1)} %broadcast_add_fusion), kind=kOutput, calls=%fused_computation.10 | convolution fusion | flops 4238868480 | bytes 15744512 | tf_op jit(solution)/shard_map/it,id->td/dot_general | solution.py:279
  442.3 5.7 prep_other.1
  448.0 432.6 %shard_map.86 = f32[37984,896]{1,0:T(8,128)} custom-call(s32[2]{0:T(128)} %compare_select_fusion.nt_ref, bf16[37984,896]{1,0:T(8,128)(2,1)} %e_ref.5, f32[37984,1536]{1,0:T(8,128)} %get-tuple-element.20.t_ref, bf16[896,1536]{1,0:T(8,128)(2,1)} %get-tuple-element.23.xto_ref, bf16[1536,896]{1,0:T(8,128)(2,1)} %get-tuple-element.24.xs_ref, ...), custom_call_target="tpu_custom_call" | custom-call | flops 313654247424 | bytes 437575680 | tf_op jit(solution)/shard_map/pallas_call | solution.py:269
  (32 shorter events, 3.8 us)
Async XLA Ops:
  7.2 415.1 %all-reduce.2.cloned.1.call-start = ((), (), s32[]{:S(2)}) async-start(), calls=%async_computation | async-start | bytes 11010048 | tf_op jit(solution)/shard_map/psum | solution.py:260
  29.6 134.1 %copy-start = (f32[1,1536]{1,0:T(1,128)S(1)}, f32[1,1536]{1,0:T(1,128)}, u32[]{:S(2)}) copy-start(f32[1,1536]{1,0:T(1,128)} %get-tuple-element.16) | copy-start | bytes 18436
  163.7 24.2 %collective-permute-start = (f32[4,1536]{1,0:T(4,128)S(1)}, f32[4,1536]{1,0:T(4,128)S(1)}, u32[]{:S(2)}, u32[]{:S(2)}) collective-permute-start(f32[4,1536]{1,0:T(4,128)S(1)} %pad_maximum_fusion), channel_id=1, source_target_pairs={{0,4},{4,0},{1,5},{5,1},{2,6},{6,2},{3,7},{7,3}} | collective-permute-start | bytes 73736 | tf_op jit(solution)/shard_map/ppermute | solution.py:242
  185.9 256.4 %collective-permute-start.1 = (f32[1536,896]{1,0:T(8,128)}, f32[1536,896]{1,0:T(8,128)}, u32[]{:S(2)}, u32[]{:S(2)}) collective-permute-start(f32[1536,896]{1,0:T(8,128)} %get-tuple-element.22), channel_id=1, source_target_pairs={{0,4},{4,0},{1,5},{5,1},{2,6},{6,2},{3,7},{7,3}} | collective-permute-start | bytes 16515080 | tf_op jit(solution)/shard_map/ppermute | solution.py:219
  190.5 123.4 %copy-start.1 = (f32[2,1536]{1,0:T(2,128)}, f32[2,1536]{1,0:T(2,128)S(1)}, u32[]{:S(2)}) copy-start(f32[2,1536]{1,0:T(2,128)S(1)} %get-tuple-element.35.lz_ref) | copy-start | bytes 36868
  190.5 123.4 %copy-start.2 = (f32[2,1536]{1,0:T(2,128)}, f32[2,1536]{1,0:T(2,128)S(1)}, u32[]{:S(2)}) copy-start(f32[2,1536]{1,0:T(2,128)S(1)} %get-tuple-element.36.ts_ref) | copy-start | bytes 36868
  314.0 3.8 copy-start.3
Sparse Core Ops, SparseCore 0:
  314.1 108.0 all-reduce.1

commit v3 on v2

v3 whole, which is shorter than its diff:
```python
import functools
import jax
import jax.numpy as jnp
from jax import lax
from jax.experimental import pallas as pl
from jax.experimental.pallas import tpu as pltpu
from jax.sharding import PartitionSpec as P

SOFT_CAP = 30.0
LOG2E = 1.4426950408889634
CAP2 = SOFT_CAP * LOG2E
VMEM_LIMIT = 60 * 1024 * 1024
TILE = 256


def norm_apply(hid_rows, gain32):
    h32 = hid_rows.astype(jnp.float32)
    inv_rms = lax.rsqrt(jnp.mean(h32 * h32, axis=-1, keepdims=True) + 1e-6)
    return h32 * inv_rms * (1.0 + gain32)


def chunks(total, size):
    return [(s, min(size, total - s)) for s in range(0, total, size)]


def widths_of(tokens):
    return (tokens - TILE, tokens) if tokens > TILE else (tokens,)


def per_width(n_tiles, tokens, body):
    for w in widths_of(tokens):
        fits = n_tiles * TILE <= tokens - TILE
        cond = True if tokens <= TILE else (fits if w < tokens else jnp.logical_not(fits))

        @pl.when(cond)
        def _():
            body(w)


def pieces(t_refs, n, nn):
    edge = t_refs[0].shape[1]
    out = []
    if n < edge:
        out.append((t_refs[0], slice(n, min(n + nn, edge)), slice(0, min(nn, edge - n)), False))
    if n + nn > edge:
        lo = max(n, edge)
        out.append((t_refs[1], slice(lo - edge, n + nn - edge), slice(lo - n, nn), True))
    return out


def row_hits(rows, cols, base, labels):
    ids = lax.broadcasted_iota(jnp.int32, (rows, cols), 0)
    return ids == (labels - base)


def prep_kernel(hid_ref, mask_ref, dig_ref, gain_ref, hc_ref, x_ref, xt_ref, x32_ref, perm_ref, lab_ref):
    tokens = hid_ref.shape[0]
    mask = mask_ref[...]
    src = lax.broadcasted_iota(jnp.int32, (tokens, tokens), 0)
    dst = lax.broadcasted_iota(jnp.int32, (tokens, tokens), 1)
    upto = jnp.where(src <= dst, 1.0, 0.0).astype(jnp.bfloat16)
    count = jnp.dot(jnp.broadcast_to(mask, (8, tokens)).astype(jnp.bfloat16), upto, preferred_element_type=jnp.float32)
    place = jnp.where(mask > 0.0, count[0:1, :] - 1.0, -1.0).astype(jnp.int32)
    perm_ref[...] = jnp.where(src == place, 1.0, 0.0).astype(jnp.bfloat16)
    hc_ref[...] = jnp.dot(perm_ref[...], hid_ref[...], preferred_element_type=jnp.float32).astype(jnp.bfloat16)
    digits = lax.dot_general(dig_ref[...], perm_ref[...], (((1,), (1,)), ((), ())), preferred_element_type=jnp.float32)
    lab_ref[...] = digits[0:1, :] + 64.0 * digits[1:2, :] + 4096.0 * digits[2:3, :]
    for m, mm in chunks(tokens, TILE):
        rows = slice(m, m + mm)
        x32 = norm_apply(hc_ref[rows, :], gain_ref[...])
        x = x32.astype(jnp.bfloat16)
        x32_ref[rows, :] = x32
        x_ref[rows, :] = x
        xt_ref[:, rows] = x.T


def other_kernel(x32_ref, x_ref, xt_ref):
    x = x32_ref[...].astype(jnp.bfloat16)
    x_ref[...] = x
    xt_ref[...] = x.T


def logits_kernel(nblk, bv, tail, nt_ref, e_ref, xt_ref, lab_ref, ta_ref, tb_ref, sum_ref, pick_ref):
    i = pl.program_id(0)
    tokens = xt_ref.shape[1]

    @pl.when(i == 0)
    def _():
        sum_ref[...] = jnp.zeros_like(sum_ref)
        pick_ref[...] = jnp.zeros_like(pick_ref)

    def body(rows, width):
        for n, nn in chunks(width, TILE):
            cols = slice(n, n + nn)
            z = jnp.dot(e_ref[:rows, :], xt_ref[:, cols], preferred_element_type=jnp.float32)
            t = jnp.tanh(z * (1.0 / SOFT_CAP))
            for ref, rc, zc, _ in pieces((ta_ref, tb_ref), n, nn):
                ref[:rows, rc] = t[:, zc]
            e = jnp.exp2(t * CAP2)
            sum_ref[:, cols] += jnp.sum(e.reshape(rows // 8, 8, nn), axis=0)
            hit = row_hits(rows, nn, i * bv, lab_ref[0:1, cols])
            pick_ref[:, cols] += jnp.sum(jnp.where(hit, t, 0.0).reshape(rows // 8, 8, nn), axis=0)

    @pl.when(i < nblk - 1)
    def _():
        per_width(nt_ref[0], tokens, functools.partial(body, bv))

    @pl.when(i == nblk - 1)
    def _():
        body(tail, tokens)


def grad_of(t, base, lab, lz, ts):
    p = jnp.exp2(t * CAP2 - lz)
    hit = row_hits(t.shape[0], t.shape[1], base, lab)
    return (jnp.where(hit, p - 1.0, p) * ts * (1.0 - t * t)).astype(jnp.bfloat16)


def own_grads(g_ref, t_refs, n_tiles, n, nn, rows, base, lab_ref, lz_ref, ts_ref):
    tokens = t_refs[0].shape[1] + t_refs[1].shape[1]
    for ref, rc, zc, last in pieces(t_refs, n, nn):
        cols = slice(n + zc.start, n + zc.stop)
        for m, mm in chunks(rows, 64):
            t = ref[m:m + mm, rc]
            if last:
                t = jnp.where(n_tiles * TILE > tokens - TILE, t, 0.0)
            g_ref[m:m + mm, cols] = grad_of(t, base + m, lab_ref[0:1, cols], lz_ref[0:1, cols], ts_ref[0:1, cols])


def grad_x_kernel(nblk, bv, tail, nt_ref, e_ref, ta_ref, tb_ref, lab_ref, lz_ref, ts_ref, gx_ref, et_ref, g_ref):
    i = pl.program_id(0)
    tokens = gx_ref.shape[1]

    @pl.when(i == 0)
    def _():
        gx_ref[...] = jnp.zeros_like(gx_ref)

    def body(rows, width):
        for m, mm in chunks(rows, 256):
            et_ref[:, m:m + mm] = e_ref[m:m + mm, :].T
        for n, nn in chunks(width, 512):
            cols = slice(n, n + nn)
            own_grads(g_ref, (ta_ref, tb_ref), nt_ref[0], n, nn, rows, i * bv, lab_ref, lz_ref, ts_ref)
            dim = gx_ref.shape[0]
            for d, dd in chunks(dim, dim if nn > TILE else dim // 2):
                gx_ref[d:d + dd, cols] += jnp.dot(
                    et_ref[d:d + dd, :rows], g_ref[:rows, cols], preferred_element_type=jnp.float32)

    @pl.when(i < nblk - 1)
    def _():
        per_width(nt_ref[0], tokens, functools.partial(body, bv))

    @pl.when(i == nblk - 1)
    def _():
        body(tail, tokens)


def grad_table_kernel(nblk, bv, tail, nt_ref, e_ref, ta_ref, tb_ref, xto_ref, xs_ref, xo_ref, lab_ref, lz_ref, ts_ref, de_ref, g_ref):
    i = pl.program_id(0)
    tokens = xto_ref.shape[1]

    def body(rows, width):
        for n, nn in chunks(width, TILE):
            cols = slice(n, n + nn)
            z = jnp.dot(e_ref[:rows, :], xto_ref[:, cols], preferred_element_type=jnp.float32)
            t = jnp.tanh(z * (1.0 / SOFT_CAP))
            g_ref[:rows, tokens + n:tokens + n + nn] = grad_of(
                t, i * bv, lab_ref[1:2, cols], lz_ref[1:2, cols], ts_ref[1:2, cols])
            own_grads(g_ref, (ta_ref, tb_ref), nt_ref[0], n, nn, rows, i * bv, lab_ref, lz_ref, ts_ref)
        de_ref[:rows, :] = (
            jnp.dot(g_ref[:rows, :width], xs_ref[:width, :], preferred_element_type=jnp.float32)
            + jnp.dot(g_ref[:rows, tokens:tokens + width], xo_ref[:width, :], preferred_element_type=jnp.float32))

    @pl.when(i < nblk - 1)
    def _():
        per_width(jnp.maximum(nt_ref[0], nt_ref[1]), tokens, functools.partial(body, bv))

    @pl.when(i == nblk - 1)
    def _():
        body(tail, tokens)


def stats_kernel(n_dp, n_tp, vocab, pack_ref, lz_ref, ts_ref, lab_ref, count_ref, loss_ref, got, send_sem, recv_sem):
    dp, tp = lax.axis_index('dp'), lax.axis_index('tp')
    me = dp * n_tp + tp
    far = [(a, b) for a in range(n_dp) for b in range(n_tp) if a or b]
    peer = lambda a, b: {'dp': lax.rem(dp + a, n_dp), 'tp': lax.rem(tp + b, n_tp)}
    barrier = pltpu.get_barrier_semaphore()
    for a, b in far:
        pl.semaphore_signal(barrier, inc=1, device_id=peer(a, b), device_id_type=pl.DeviceIdType.MESH)
    pl.semaphore_wait(barrier, len(far))
    copies = []
    for k, (a, b) in enumerate(far):
        copies.append(pltpu.make_async_remote_copy(
            src_ref=pack_ref, dst_ref=got.at[me], send_sem=send_sem.at[k], recv_sem=recv_sem.at[k],
            device_id=peer(a, b), device_id_type=pl.DeviceIdType.MESH))
        copies[-1].start()
    got[me] = pack_ref[...]
    for c in copies:
        c.wait()
    zs, picks, masks, labs = [], [], [], []
    for d in range(n_dp):
        rows = [got[d * n_tp + k] for k in range(n_tp)]
        total = functools.reduce(lambda u, v: u + v, rows)
        live = rows[0][2:3, :] > 0.0
        masks.append(rows[0][2:3, :])
        labs.append(rows[0][3:4, :])
        zs.append(jnp.where(live, jnp.log(jnp.where(live, total[0:1, :], 1.0)), 0.0))
        picks.append(jnp.where(live, SOFT_CAP * total[1:2, :], 0.0))
    counts = [jnp.sum(m, axis=1, keepdims=True) for m in masks]
    n = jnp.maximum(functools.reduce(lambda u, v: u + v, counts), 1.0)
    losses = [jnp.sum(z - p, axis=1, keepdims=True) for z, p in zip(zs, picks)]
    loss = functools.reduce(lambda u, v: u + v, losses) / n
    loss_ref[...] = jnp.broadcast_to(loss, loss_ref.shape)
    first = dp == 0
    for r in range(n_dp):
        def pick(v):
            return jnp.where(first, v[r], v[n_dp - 1 - r])

        lz_ref[r:r + 1, :] = pick(zs) * LOG2E
        ts_ref[r:r + 1, :] = pick(masks) / n
        lab_ref[r:r + 1, :] = pick(labs).astype(jnp.int32) - tp * vocab
        count_ref[r:r + 1, :] = jnp.broadcast_to(pick(counts), (1, count_ref.shape[1])).astype(jnp.int32)


def whole(shape):
    return pl.BlockSpec(shape, lambda *_: (0,) * len(shape))


def blocks(rows, cols):
    return pl.BlockSpec((rows, cols), lambda i, *_: (i, 0))


def parked(rows, cols, tokens):
    return pl.BlockSpec((rows, cols), lambda i, nt: (jnp.where(nt[0] * TILE > tokens - TILE, i, 0), 0))


def params(**kw):
    return pltpu.CompilerParams(vmem_limit_bytes=VMEM_LIMIT, **kw)


def table_call(kernel, vocab, rows, in_specs, out_specs, out_shape, scratch, cost):
    nblk = pl.cdiv(vocab, rows)
    tail = vocab - (nblk - 1) * rows
    return pl.pallas_call(
        functools.partial(kernel, nblk, rows, tail),
        grid_spec=pltpu.PrefetchScalarGridSpec(
            num_scalar_prefetch=1, grid=(nblk,), in_specs=in_specs, out_specs=out_specs, scratch_shapes=scratch),
        out_shape=out_shape,
        compiler_params=params(dimension_semantics=("arbitrary",)),
        cost_estimate=cost,
    )


def solution(mesh):
    n_dp, n_tp = mesh.shape['dp'], mesh.shape['tp']
    swap = [(i, n_dp - 1 - i) for i in range(n_dp)]

    def local_step(hidden, norm_w, embed_table, labels, loss_mask):
        batch_rows, seq_len, dim = hidden.shape
        vocab = embed_table.shape[0]
        tokens = batch_rows * seq_len
        hid_rows = hidden.reshape(tokens, dim)
        mask_rows = loss_mask.reshape(1, tokens).astype(jnp.float32)
        gain = norm_w.astype(jnp.float32)
        lab_rows = labels.reshape(tokens)
        digits = jnp.stack([lab_rows & 63, (lab_rows >> 6) & 63, lab_rows >> 12] + [jnp.zeros_like(lab_rows)] * 5)
        f32, b16 = jnp.float32, jnp.bfloat16
        shape = jax.ShapeDtypeStruct
        hid_c, x_own, xt_own, x32, perm, lab_c = pl.pallas_call(
            prep_kernel,
            out_shape=[shape((tokens, dim), b16), shape((tokens, dim), b16), shape((dim, tokens), b16),
                       shape((tokens, dim), f32), shape((tokens, tokens), b16), shape((1, tokens), f32)],
            compiler_params=params(),
            name="prep",
        )(hid_rows, mask_rows, digits.astype(b16), gain.reshape(1, dim))
        other32 = lax.ppermute(x32, 'dp', swap)
        count = jnp.sum(mask_rows)
        mask_c = (jnp.arange(tokens, dtype=jnp.int32)[None, :] < count.astype(jnp.int32)).astype(f32)
        base = lax.axis_index('tp') * vocab
        lab_own = jnp.broadcast_to(lab_c.astype(jnp.int32) - base, (8, tokens))
        nt_own = pl.cdiv(count.astype(jnp.int32), TILE).reshape(1)

        row = whole((8, tokens))
        edge = tokens - TILE
        flops = 2 * tokens * vocab * dim
        elems = vocab * tokens

        bv = 1024
        t_a, t_b, sums, picks = table_call(
            logits_kernel, vocab, bv,
            [blocks(bv, dim), whole((dim, tokens)), row],
            [blocks(bv, edge), parked(bv, TILE, tokens), row, row],
            [shape((vocab, edge), f32), shape((vocab, TILE), f32), shape((8, tokens), f32), shape((8, tokens), f32)], [],
            pl.CostEstimate(flops=flops, bytes_accessed=elems * 4 + vocab * dim * 2, transcendentals=2 * elems),
        )(nt_own, embed_table, xt_own, lab_own)

        pack = jnp.concatenate([jnp.sum(sums, axis=0, keepdims=True), jnp.sum(picks, axis=0, keepdims=True), mask_c, lab_c,
                                jnp.zeros((4, tokens), f32)], axis=0)
        n_dev = n_dp * n_tp
        lz, ts, lab, counts, loss = pl.pallas_call(
            functools.partial(stats_kernel, n_dp, n_tp, vocab),
            out_shape=[shape((8, tokens), f32), shape((8, tokens), f32), shape((8, tokens), jnp.int32),
                       shape((8, 128), jnp.int32), shape((8, 128), f32)],
            in_specs=[pl.BlockSpec(memory_space=pltpu.VMEM)],
            out_specs=[pl.BlockSpec(memory_space=pltpu.VMEM)] * 5,
            scratch_shapes=[pltpu.VMEM((n_dev, 8, tokens), f32), pltpu.SemaphoreType.DMA((n_dev - 1,)),
                            pltpu.SemaphoreType.DMA((n_dev - 1,))],
            compiler_params=params(collective_id=0, has_side_effects=True),
            name="stats",
        )(pack)
        mean_loss = loss[0, 0]
        nt_both = pl.cdiv(counts[0:2, 0], TILE)

        bx = 1024
        gxt = table_call(
            grad_x_kernel, vocab, bx,
            [blocks(bx, dim), blocks(bx, edge), parked(bx, TILE, tokens), row, row, row], whole((dim, tokens)), shape((dim, tokens), f32),
            [pltpu.VMEM((dim, bx), b16), pltpu.VMEM((bx, tokens), b16)],
            pl.CostEstimate(flops=flops, bytes_accessed=elems * 4 + vocab * dim * 2, transcendentals=elems),
        )(nt_own, embed_table, t_a, t_b, lab, lz, ts)
        grad_xt = lax.psum(gxt, 'tp')

        x_other, xt_other = pl.pallas_call(
            other_kernel, out_shape=[shape((tokens, dim), b16), shape((dim, tokens), b16)],
            compiler_params=params(), name="prep_other",
        )(other32)

        ts_late, _ = lax.optimization_barrier((ts, gxt[0, 0]))
        bt = 1024
        grad_table = table_call(
            grad_table_kernel, vocab, bt,
            [blocks(bt, dim), blocks(bt, edge), parked(bt, TILE, tokens), whole((dim, tokens)), whole((tokens, dim)),
             whole((tokens, dim)), row, row, row],
            blocks(bt, dim), shape((vocab, dim), f32), [pltpu.VMEM((bt, 2 * tokens), b16)],
            pl.CostEstimate(flops=3 * flops, bytes_accessed=elems * 4 + vocab * dim * 6, transcendentals=3 * elems),
        )(nt_both, embed_table, t_a, t_b, xt_other, x_own, x_other, lab, lz, ts_late)

        _, norm_back = jax.vjp(norm_apply, hid_c, gain)
        grad_rows, grad_gain = norm_back(grad_xt.T)
        grad_rows = jnp.einsum('it,id->td', perm, grad_rows, preferred_element_type=f32).astype(b16)
        grad_gain = lax.psum(grad_gain, 'dp')
        return mean_loss, grad_rows.reshape(batch_rows, seq_len, dim), grad_gain, grad_table

    return jax.shard_map(local_step, mesh=mesh, in_specs=(P('dp', None, None), P(None), P('tp', None), P('dp', None), P('dp', None)), out_specs=(P(), P('dp', None, None), P(None), P('tp', None)), check_vma=False)
```

time: 896 us -> 956 us (1.067)
  Pallas kernels: 695 us -> 784 us
  starting transfers between devices: 22.2 us -> 3.38 us
  blocking collectives: 18.5 us -> 5.52 us
    pallas_call x2 -> x3, Pallas kernels: 555 us -> 625 us  [the longest x1 472 us: local_step(): table_call(grad_table_kernel, vocab, bt, [blocks(bt, dim), blocks(bt, edg...]
    ppermute x1 -> x0, starting transfers between devices: 22.1 us -> none  [local_step(): pack_other = lax.ppermute(pack_own, 'dp', swap)]
    pallas_call x1, Pallas kernels: 119 us -> 138 us  [local_step(): table_call(logits_kernel, vocab, bv, [blocks(bv, dim), whole((dim, tokens...]
    psum x1 -> x0, blocking collectives: 13 us -> none  [local_step(): lax.psum(jnp.stack([jnp.sum(sums, axis=0), jnp.sum(picks, axis=0)]), 'tp')]
  transfers between devices with their start and end apart: 3 -> 2, of which waited for: 2 -> 1; matrix products, arithmetic and copies ran while one was open for 3% -> 3% of each run, Pallas kernels for 14% -> 31%
where the time goes in v3:
time: 956 us; the launch traced here: 949 us
  Pallas kernels  784 us (82%)
  waiting for transfers between devices  110 us (12%)
  between operations  15.2 us (2%)
  other arithmetic  11.2 us (1%)
  matrix products  10.1 us (1%)
    pallas_call x1, Pallas kernels, local_step(): table_call(grad_table_kernel, vocab, bt, [blocks(bt, dim), blocks(bt, edg...  472 us
    pallas_call x1, Pallas kernels, local_step(): table_call(logits_kernel, vocab, bv, [blocks(bv, dim), whole((dim, tokens...  138 us
    pallas_call x1, Pallas kernels, local_step(): table_call(grad_x_kernel, vocab, bx, [blocks(bx, dim), blocks(bx, edge),...  115 us
    psum x1, waiting for transfers between devices, local_step(): grad_xt = lax.psum(gxt, 'tp')  110 us
    pallas_call x1, Pallas kernels, local_step(): pl.pallas_call(functools.partial(stats_kernel, n_dp, n_tp, vocab), out_sh...  38.3 us
  transfers between devices with their start and end apart: 2, of which 1 were waited for; matrix products, arithmetic and copies ran while one was open for 3% of the time, Pallas kernels for 31%

profile of v3, /device:TPU:0, one launch (start us, length us, event | category | flops | bytes accessed | tf_op | source)
XLA Modules:
  0.0 948.7 jit_solution(13994293744123693315)
XLA Ops:
  7.2 0.7 convert_bitcast_fusion
  8.5 0.7 fusion.12
  9.3 1.3 reshape.115.gain_ref
  10.5 0.7 stack.11.dig_ref
  11.2 15.1 %prep.1 = (bf16[1536,896]{1,0:T(8,128)(2,1)}, bf16[1536,896]{1,0:T(8,128)(2,1)}, bf16[896,1536]{1,0:T(8,128)(2,1)}, f32[1536,896]{1,0:T(8,128)}, bf16[1536,1536]{1,0:T(8,128)(2,1)}, /*index=5*/f32[1,1536]{1,0:T(1,128)}) custom-call(bf16[1536,896]{1,0:T(8,128)(2,1)} %bitcast.23, f32[1,1536]{1,0:T(1,128)} %bitcast.27, bf16[8,1536]{1,0:T(8,128)(2,1)} %stack.11.dig_ref, ...), custom_call_target="tpu_custom_call" | custom-call | tf_op jit(solution)/shard_map/prep/pallas_call | solution.py:270
  26.3 3.3 collective-permute-start
  29.7 1.3 convert_reduce_fusion
  31.7 0.7 subtract_reduce_fusion
  32.4 0.6 broadcast_in_dim.23.lab_ref
  33.0 138.2 %shard_map.84 = (f32[37984,1280]{1,0:T(8,128)}, f32[37984,256]{1,0:T(8,128)}, f32[8,1536]{1,0:T(8,128)}, f32[8,1536]{1,0:T(8,128)}) custom-call(s32[1]{0:T(128)} %bitcast.nt_ref, bf16[37984,896]{1,0:T(8,128)(2,1)} %e_ref.5, bf16[896,1536]{1,0:T(8,128)(2,1)} %get-tuple-element.21.xt_ref, s32[8,1536]{1,0:T(8,128)} %broadcast_in_dim.23.lab_ref), custom_call_target="tpu_custom_call" | custom-call | flops 104551415808 | bytes 301441024 | tf_op jit(solution)/shard_map/pallas_call | solution.py:290
  171.2 0.8 reduce_sum.55
  172.0 0.8 reduce_sum.64
  172.9 0.7 concatenate.3.pack_ref
  173.5 38.3 %stats.1 = (f32[8,1536]{1,0:T(8,128)}, f32[8,1536]{1,0:T(8,128)}, s32[8,1536]{1,0:T(8,128)}, s32[8,128]{1,0:T(8,128)}, f32[8,128]{1,0:T(8,128)}) custom-call(f32[8,1536]{1,0:T(8,128)} %concatenate.3.pack_ref), custom_call_target="tpu_custom_call" | custom-call | tf_op jit(solution)/shard_map/stats/pallas_call | solution.py:301
  211.9 114.9 %shard_map.85 = f32[896,1536]{1,0:T(8,128)} custom-call(s32[1]{0:T(128)} %bitcast.nt_ref, bf16[37984,896]{1,0:T(8,128)(2,1)} %e_ref.5, f32[37984,1280]{1,0:T(8,128)} %get-tuple-element.27.ta_ref, f32[37984,256]{1,0:T(8,128)} %get-tuple-element.28.tb_ref, s32[8,1536]{1,0:T(8,128)} %get-tuple-element.29.lab_ref, f32[8,1536]{1,0:T(8,128)} %get-tuple-element.30.lz_ref, ...), custom_call_target="tpu_custom_call" | custom-call | flops 104551415808 | bytes 301441024 | tf_op jit(solution)/shard_map/pallas_call | solution.py:316
  326.8 1.2 slice.7
  328.0 3.3 copy.10
  331.3 0.8 add_reduce_fusion
  333.3 110.5 %all-reduce.2.cloned.1.call-done = f32[1536,896]{0,1:T(8,128)} async-done(((f32[1536,896]{0,1:T(8,128)}), f32[1536,896]{0,1:T(8,128)}) %all-reduce.2.cloned.1.call-update) | async-done | bytes 5505040 | tf_op jit(solution)/shard_map/psum | solution.py:322
  443.8 4.1 fusion.4
  447.9 5.5 psum.15
  453.4 10.1 %convolution_convert_fusion = bf16[1536,896]{1,0:T(8,128)(2,1)} fusion(bf16[1536,1536]{1,0:T(8,128)(2,1)} %get-tuple-element.26, bf16[1536,896]{0,1:T(8,128)(2,1)S(1)} %copy.10, f32[1536,896]{0,1:T(8,128)} %all-reduce.2.cloned.1.call-done, f32[1536]{0:T(1024)S(1)} %multiply_multiply_fusion, f32[1536]{0:T(1024)S(1)} %fusion.9, f32[896]{0:T(1024)S(1)} %broadcast_add_fusion), kind=kOutput, calls=%fused_computation.10 | convolution fusion | flops 4238868480 | bytes 15744512 | tf_op jit(solution)/shard_map/it,id->td/dot_general | solution.py:341
  463.6 5.7 prep_other.1
  469.3 472.2 %shard_map.86 = f32[37984,896]{1,0:T(8,128)} custom-call(s32[2]{0:T(128)} %compare_select_fusion.nt_ref, bf16[37984,896]{1,0:T(8,128)(2,1)} %e_ref.5, f32[37984,1280]{1,0:T(8,128)} %get-tuple-element.27.ta_ref, f32[37984,256]{1,0:T(8,128)} %get-tuple-element.28.tb_ref, bf16[896,1536]{1,0:T(8,128)(2,1)} %get-tuple-element.35.xto_ref, ...), custom_call_target="tpu_custom_call" | custom-call | flops 313654247424 | bytes 437575680 | tf_op jit(solution)/shard_map/pallas_call | solution.py:331
  (22 shorter events, 2.0 us)
Async XLA Ops:
  7.2 436.6 %all-reduce.2.cloned.1.call-start = ((), (), s32[]{:S(2)}) async-start(), calls=%async_computation | async-start | bytes 11010048 | tf_op jit(solution)/shard_map/psum | solution.py:322
  26.3 437.2 %collective-permute-start = (f32[1536,896]{1,0:T(8,128)}, f32[1536,896]{1,0:T(8,128)}, u32[]{:S(2)}, u32[]{:S(2)}) collective-permute-start(f32[1536,896]{1,0:T(8,128)} %get-tuple-element.34), channel_id=1, source_target_pairs={{0,4},{4,0},{1,5},{5,1},{2,6},{6,2},{3,7},{7,3}} | collective-permute-start | bytes 16515080 | tf_op jit(solution)/shard_map/ppermute | solution.py:277
  33.0 139.9 %copy-start = (f32[1,1536]{1,0:T(1,128)S(1)}, f32[1,1536]{1,0:T(1,128)}, u32[]{:S(2)}) copy-start(f32[1,1536]{1,0:T(1,128)} %get-tuple-element.22) | copy-start | bytes 18436
  326.8 5.9 copy-start.1
Sparse Core Ops, SparseCore 0:
  326.9 116.8 all-reduce.1

commit v4 on v3

--- a/solution.py
+++ b/solution.py
@@ -53,7 +53,7 @@
     return ids == (labels - base)
 
 
-def prep_kernel(hid_ref, mask_ref, dig_ref, gain_ref, hc_ref, x_ref, xt_ref, x32_ref, perm_ref, lab_ref):
+def prep_kernel(hid_ref, mask_ref, dig_ref, gain_ref, hc_ref, xt_ref, x32_ref, perm_ref, lab_ref):
     tokens = hid_ref.shape[0]
     mask = mask_ref[...]
     src = lax.broadcasted_iota(jnp.int32, (tokens, tokens), 0)
@@ -68,16 +68,12 @@
     for m, mm in chunks(tokens, TILE):
         rows = slice(m, m + mm)
         x32 = norm_apply(hc_ref[rows, :], gain_ref[...])
-        x = x32.astype(jnp.bfloat16)
         x32_ref[rows, :] = x32
-        x_ref[rows, :] = x
-        xt_ref[:, rows] = x.T
-
-
-def other_kernel(x32_ref, x_ref, xt_ref):
-    x = x32_ref[...].astype(jnp.bfloat16)
-    x_ref[...] = x
-    xt_ref[...] = x.T
+        xt_ref[:, rows] = x32.astype(jnp.bfloat16).T
+
+
+def other_kernel(x32_ref, xt_ref):
+    xt_ref[...] = x32_ref[...].astype(jnp.bfloat16).T
 
 
 def logits_kernel(nblk, bv, tail, nt_ref, e_ref, xt_ref, lab_ref, ta_ref, tb_ref, sum_ref, pick_ref):
@@ -90,16 +86,17 @@
         pick_ref[...] = jnp.zeros_like(pick_ref)
 
     def body(rows, width):
-        for n, nn in chunks(width, TILE):
-            cols = slice(n, n + nn)
-            z = jnp.dot(e_ref[:rows, :], xt_ref[:, cols], preferred_element_type=jnp.float32)
-            t = jnp.tanh(z * (1.0 / SOFT_CAP))
-            for ref, rc, zc, _ in pieces((ta_ref, tb_ref), n, nn):
-                ref[:rows, rc] = t[:, zc]
-            e = jnp.exp2(t * CAP2)
-            sum_ref[:, cols] += jnp.sum(e.reshape(rows // 8, 8, nn), axis=0)
-            hit = row_hits(rows, nn, i * bv, lab_ref[0:1, cols])
-            pick_ref[:, cols] += jnp.sum(jnp.where(hit, t, 0.0).reshape(rows // 8, 8, nn), axis=0)
+        for m, mm in chunks(rows, 256):
+            for n, nn in chunks(width, 512):
+                cols = slice(n, n + nn)
+                z = jnp.dot(e_ref[m:m + mm, :], xt_ref[:, cols], preferred_element_type=jnp.float32)
+                t = jnp.tanh(z * (1.0 / SOFT_CAP))
+                for ref, rc, zc, _ in pieces((ta_ref, tb_ref), n, nn):
+                    ref[m:m + mm, rc] = t[:, zc]
+                e = jnp.exp2(t * CAP2)
+                sum_ref[:, cols] += jnp.sum(e.reshape(mm // 8, 8, nn), axis=0)
+                hit = row_hits(mm, nn, i * bv + m, lab_ref[0:1, cols])
+                pick_ref[:, cols] += jnp.sum(jnp.where(hit, t, 0.0).reshape(mm // 8, 8, nn), axis=0)
 
     @pl.when(i < nblk - 1)
     def _():
@@ -155,21 +152,29 @@
         body(tail, tokens)
 
 
-def grad_table_kernel(nblk, bv, tail, nt_ref, e_ref, ta_ref, tb_ref, xto_ref, xs_ref, xo_ref, lab_ref, lz_ref, ts_ref, de_ref, g_ref):
+def grad_table_kernel(nblk, bv, tail, nt_ref, e_ref, ta_ref, tb_ref, xts_ref, xto_ref, lab_ref, lz_ref, ts_ref, de_ref, g_ref):
     i = pl.program_id(0)
     tokens = xto_ref.shape[1]
 
+    def over_tokens(a, b):
+        return lax.dot_general(a, b, (((1,), (1,)), ((), ())), preferred_element_type=jnp.float32)
+
     def body(rows, width):
-        for n, nn in chunks(width, TILE):
+        for n, nn in chunks(width, 512):
             cols = slice(n, n + nn)
-            z = jnp.dot(e_ref[:rows, :], xto_ref[:, cols], preferred_element_type=jnp.float32)
-            t = jnp.tanh(z * (1.0 / SOFT_CAP))
-            g_ref[:rows, tokens + n:tokens + n + nn] = grad_of(
-                t, i * bv, lab_ref[1:2, cols], lz_ref[1:2, cols], ts_ref[1:2, cols])
+            for m, mm in chunks(rows, 256):
+                z = jnp.dot(e_ref[m:m + mm, :], xto_ref[:, cols], preferred_element_type=jnp.float32)
+                t = jnp.tanh(z * (1.0 / SOFT_CAP))
+                g_ref[m:m + mm, tokens + n:tokens + n + nn] = grad_of(
+                    t, i * bv + m, lab_ref[1:2, cols], lz_ref[1:2, cols], ts_ref[1:2, cols])
             own_grads(g_ref, (ta_ref, tb_ref), nt_ref[0], n, nn, rows, i * bv, lab_ref, lz_ref, ts_ref)
-        de_ref[:rows, :] = (
-            jnp.dot(g_ref[:rows, :width], xs_ref[:width, :], preferred_element_type=jnp.float32)
-            + jnp.dot(g_ref[:rows, tokens:tokens + width], xo_ref[:width, :], preferred_element_type=jnp.float32))
+        sides = [(xts_ref[:, :width], g_ref[:rows, :width]), (xto_ref[:, :width], g_ref[:rows, tokens:tokens + width])]
+        if rows % 128 == 0:
+            (xa, ga), (xb, gb) = sides
+            de_ref[:rows, :] = (over_tokens(xa, ga) + over_tokens(xb, gb)).T
+        else:
+            (xa, ga), (xb, gb) = sides
+            de_ref[:rows, :] = over_tokens(ga, xa) + over_tokens(gb, xb)
 
     @pl.when(i < nblk - 1)
     def _():
@@ -267,10 +272,10 @@
         digits = jnp.stack([lab_rows & 63, (lab_rows >> 6) & 63, lab_rows >> 12] + [jnp.zeros_like(lab_rows)] * 5)
         f32, b16 = jnp.float32, jnp.bfloat16
         shape = jax.ShapeDtypeStruct
-        hid_c, x_own, xt_own, x32, perm, lab_c = pl.pallas_call(
+        hid_c, xt_own, x32, perm, lab_c = pl.pallas_call(
             prep_kernel,
-            out_shape=[shape((tokens, dim), b16), shape((tokens, dim), b16), shape((dim, tokens), b16),
-                       shape((tokens, dim), f32), shape((tokens, tokens), b16), shape((1, tokens), f32)],
+            out_shape=[shape((tokens, dim), b16), shape((dim, tokens), b16), shape((tokens, dim), f32),
+                       shape((tokens, tokens), b16), shape((1, tokens), f32)],
             compiler_params=params(),
             name="prep",
         )(hid_rows, mask_rows, digits.astype(b16), gain.reshape(1, dim))
@@ -321,8 +326,8 @@
         )(nt_own, embed_table, t_a, t_b, lab, lz, ts)
         grad_xt = lax.psum(gxt, 'tp')
 
-        x_other, xt_other = pl.pallas_call(
-            other_kernel, out_shape=[shape((tokens, dim), b16), shape((dim, tokens), b16)],
+        xt_other = pl.pallas_call(
+            other_kernel, out_shape=shape((dim, tokens), b16),
             compiler_params=params(), name="prep_other",
         )(other32)
 
@@ -330,11 +335,11 @@
         bt = 1024
         grad_table = table_call(
             grad_table_kernel, vocab, bt,
-            [blocks(bt, dim), blocks(bt, edge), parked(bt, TILE, tokens), whole((dim, tokens)), whole((tokens, dim)),
-             whole((tokens, dim)), row, row, row],
+            [blocks(bt, dim), blocks(bt, edge), parked(bt, TILE, tokens), whole((dim, tokens)), whole((dim, tokens)),
+             row, row, row],
             blocks(bt, dim), shape((vocab, dim), f32), [pltpu.VMEM((bt, 2 * tokens), b16)],
             pl.CostEstimate(flops=3 * flops, bytes_accessed=elems * 4 + vocab * dim * 6, transcendentals=3 * elems),
-        )(nt_both, embed_table, t_a, t_b, xt_other, x_own, x_other, lab, lz, ts_late)
+        )(nt_both, embed_table, t_a, t_b, xt_own, xt_other, lab, lz, ts_late)
 
         _, norm_back = jax.vjp(norm_apply, hid_c, gain)
         grad_rows, grad_gain = norm_back(grad_xt.T)

time: 956 us -> 863 us (0.903)
  Pallas kernels: 784 us -> 691 us
    pallas_call x1, Pallas kernels: 472 us -> 403 us  [local_step(): table_call(grad_table_kernel, vocab, bt, [blocks(bt, dim), blocks(bt, edg...]
    pallas_call x1, Pallas kernels: 138 us -> 125 us  [local_step(): table_call(logits_kernel, vocab, bv, [blocks(bv, dim), whole((dim, tokens...]
  transfers between devices with their start and end apart: 2 -> 2, of which waited for: 1 -> 1; matrix products, arithmetic and copies ran while one was open for 3% -> 3% of each run, Pallas kernels for 31% -> 32%
where the time goes in v4:
time: 863 us; the launch traced here: 856 us
  Pallas kernels  691 us (80%)
  waiting for transfers between devices  110 us (13%)
  between operations  15.2 us (2%)
  other arithmetic  11.3 us (1%)
  matrix products  10.3 us (1%)
    pallas_call x1, Pallas kernels, local_step(): table_call(grad_table_kernel, vocab, bt, [blocks(bt, dim), blocks(bt, edg...  403 us
    pallas_call x1, Pallas kernels, local_step(): table_call(logits_kernel, vocab, bv, [blocks(bv, dim), whole((dim, tokens...  125 us
    pallas_call x1, Pallas kernels, local_step(): table_call(grad_x_kernel, vocab, bx, [blocks(bx, dim), blocks(bx, edge),...  115 us
    psum x1, waiting for transfers between devices, local_step(): grad_xt = lax.psum(gxt, 'tp')  110 us
    pallas_call x1, Pallas kernels, local_step(): pl.pallas_call(functools.partial(stats_kernel, n_dp, n_tp, vocab), out_sh...  30 us
  transfers between devices with their start and end apart: 2, of which 1 were waited for; matrix products, arithmetic and copies ran while one was open for 3% of the time, Pallas kernels for 32%

profile of v4, /device:TPU:0, one launch (start us, length us, event | category | flops | bytes accessed | tf_op | source)
XLA Modules:
  0.0 855.9 jit_solution(16923202833252329337)
XLA Ops:
  7.2 0.7 convert_bitcast_fusion
  8.5 0.7 fusion.12
  9.3 1.3 reshape.115.gain_ref
  10.5 0.6 stack.11.dig_ref
  11.2 13.1 %prep.1 = (bf16[1536,896]{1,0:T(8,128)(2,1)}, bf16[896,1536]{1,0:T(8,128)(2,1)}, f32[1536,896]{1,0:T(8,128)}, bf16[1536,1536]{1,0:T(8,128)(2,1)}, f32[1,1536]{1,0:T(1,128)}) custom-call(bf16[1536,896]{1,0:T(8,128)(2,1)} %bitcast.23, f32[1,1536]{1,0:T(1,128)} %bitcast.27, bf16[8,1536]{1,0:T(8,128)(2,1)} %stack.11.dig_ref, f32[1,896]{1,0:T(1,128)} %reshape.115.gain_ref), custom_call_target="tpu_custom_call" | custom-call | tf_op jit(solution)/shard_map/prep/pallas_call | solution.py:275
  24.3 3.3 collective-permute-start
  27.6 1.3 convert_reduce_fusion
  29.6 0.7 subtract_reduce_fusion
  30.3 0.6 broadcast_in_dim.23.lab_ref
  31.0 125.1 %shard_map.84 = (f32[37984,1280]{1,0:T(8,128)}, f32[37984,256]{1,0:T(8,128)}, f32[8,1536]{1,0:T(8,128)}, f32[8,1536]{1,0:T(8,128)}) custom-call(s32[1]{0:T(128)} %bitcast.nt_ref, bf16[37984,896]{1,0:T(8,128)(2,1)} %e_ref.5, bf16[896,1536]{1,0:T(8,128)(2,1)} %get-tuple-element.18.xt_ref.xts_ref, s32[8,1536]{1,0:T(8,128)} %broadcast_in_dim.23.lab_ref), custom_call_target="tpu_custom_call" | custom-call | flops 104551415808 | bytes 301441024 | tf_op jit(solution)/shard_map/pallas_call | solution.py:295
  156.1 0.8 reduce_sum.55
  156.9 0.8 reduce_sum.64
  157.8 0.7 concatenate.3.pack_ref
  158.4 30.0 %stats.1 = (f32[8,1536]{1,0:T(8,128)}, f32[8,1536]{1,0:T(8,128)}, s32[8,1536]{1,0:T(8,128)}, s32[8,128]{1,0:T(8,128)}, f32[8,128]{1,0:T(8,128)}) custom-call(f32[8,1536]{1,0:T(8,128)} %concatenate.3.pack_ref), custom_call_target="tpu_custom_call" | custom-call | tf_op jit(solution)/shard_map/stats/pallas_call | solution.py:306
  188.5 114.9 %shard_map.85 = f32[896,1536]{1,0:T(8,128)} custom-call(s32[1]{0:T(128)} %bitcast.nt_ref, bf16[37984,896]{1,0:T(8,128)(2,1)} %e_ref.5, f32[37984,1280]{1,0:T(8,128)} %get-tuple-element.24.ta_ref, f32[37984,256]{1,0:T(8,128)} %get-tuple-element.25.tb_ref, s32[8,1536]{1,0:T(8,128)} %get-tuple-element.26.lab_ref, f32[8,1536]{1,0:T(8,128)} %get-tuple-element.27.lz_ref, ...), custom_call_target="tpu_custom_call" | custom-call | flops 104551415808 | bytes 301441024 | tf_op jit(solution)/shard_map/pallas_call | solution.py:321
  303.4 1.2 slice.7
  304.6 3.3 copy.10
  307.9 0.8 add_reduce_fusion
  309.9 110.5 %all-reduce.2.cloned.1.call-done = f32[1536,896]{0,1:T(8,128)} async-done(((f32[1536,896]{0,1:T(8,128)}), f32[1536,896]{0,1:T(8,128)}) %all-reduce.2.cloned.1.call-update) | async-done | bytes 5505040 | tf_op jit(solution)/shard_map/psum | solution.py:327
  420.4 4.2 fusion.4
  424.6 5.5 psum.15
  430.1 10.3 %convolution_convert_fusion = bf16[1536,896]{1,0:T(8,128)(2,1)} fusion(bf16[1536,1536]{1,0:T(8,128)(2,1)} %get-tuple-element.23, bf16[1536,896]{0,1:T(8,128)(2,1)S(1)} %copy.10, f32[1536,896]{0,1:T(8,128)} %all-reduce.2.cloned.1.call-done, f32[1536]{0:T(1024)S(1)} %multiply_multiply_fusion, f32[1536]{0:T(1024)S(1)} %fusion.9, f32[896]{0:T(1024)S(1)} %broadcast_add_fusion), kind=kOutput, calls=%fused_computation.10 | convolution fusion | flops 4238868480 | bytes 15744512 | tf_op jit(solution)/shard_map/it,id->td/dot_general | solution.py:346
  440.4 4.8 prep_other.1.xto_ref
  445.2 403.5 %shard_map.86 = f32[37984,896]{1,0:T(8,128)} custom-call(s32[2]{0:T(128)} %compare_select_fusion.nt_ref, bf16[37984,896]{1,0:T(8,128)(2,1)} %e_ref.5, f32[37984,1280]{1,0:T(8,128)} %get-tuple-element.24.ta_ref, f32[37984,256]{1,0:T(8,128)} %get-tuple-element.25.tb_ref, bf16[896,1536]{1,0:T(8,128)(2,1)} %get-tuple-element.18.xt_ref.xts_ref, ...), custom_call_target="tpu_custom_call" | custom-call | flops 313654247424 | bytes 437575680 | tf_op jit(solution)/shard_map/pallas_call | solution.py:336
  (22 shorter events, 2.0 us)
Async XLA Ops:
  7.2 413.2 %all-reduce.2.cloned.1.call-start = ((), (), s32[]{:S(2)}) async-start(), calls=%async_computation | async-start | bytes 11010048 | tf_op jit(solution)/shard_map/psum | solution.py:327
  24.3 416.1 %collective-permute-start = (f32[1536,896]{1,0:T(8,128)}, f32[1536,896]{1,0:T(8,128)}, u32[]{:S(2)}, u32[]{:S(2)}) collective-permute-start(f32[1536,896]{1,0:T(8,128)} %get-tuple-element.31), channel_id=1, source_target_pairs={{0,4},{4,0},{1,5},{5,1},{2,6},{6,2},{3,7},{7,3}} | collective-permute-start | bytes 16515080 | tf_op jit(solution)/shard_map/ppermute | solution.py:282
  31.0 126.8 %copy-start = (f32[1,1536]{1,0:T(1,128)S(1)}, f32[1,1536]{1,0:T(1,128)}, u32[]{:S(2)}) copy-start(f32[1,1536]{1,0:T(1,128)} %get-tuple-element.19) | copy-start | bytes 18436
  303.3 5.9 copy-start.1
Sparse Core Ops, SparseCore 0:
  303.5 116.8 all-reduce.1

commit v5 on v4

--- a/solution.py
+++ b/solution.py
@@ -17,6 +17,12 @@
     h32 = hid_rows.astype(jnp.float32)
     inv_rms = lax.rsqrt(jnp.mean(h32 * h32, axis=-1, keepdims=True) + 1e-6)
     return h32 * inv_rms * (1.0 + gain32)
+
+
+def norm_apply_t(hid_cols, gain32):
+    h32 = hid_cols.astype(jnp.float32)
+    inv_rms = lax.rsqrt(jnp.mean(h32 * h32, axis=0, keepdims=True) + 1e-6)
+    return h32 * inv_rms * (1.0 + gain32[:, None])
 
 
 def chunks(total, size):
@@ -53,7 +59,7 @@
     return ids == (labels - base)
 
 
-def prep_kernel(hid_ref, mask_ref, dig_ref, gain_ref, hc_ref, xt_ref, x32_ref, perm_ref, lab_ref):
+def prep_kernel(hid_ref, mask_ref, dig_ref, gain_ref, hct_ref, xt_ref, x32_ref, perm_ref, lab_ref, hc_ref):
     tokens = hid_ref.shape[0]
     mask = mask_ref[...]
     src = lax.broadcasted_iota(jnp.int32, (tokens, tokens), 0)
@@ -70,6 +76,7 @@
         x32 = norm_apply(hc_ref[rows, :], gain_ref[...])
         x32_ref[rows, :] = x32
         xt_ref[:, rows] = x32.astype(jnp.bfloat16).T
+        hct_ref[:, rows] = hc_ref[rows, :].T
 
 
 def other_kernel(x32_ref, xt_ref):
@@ -159,16 +166,19 @@
     def over_tokens(a, b):
         return lax.dot_general(a, b, (((1,), (1,)), ((), ())), preferred_element_type=jnp.float32)
 
-    def body(rows, width):
-        for n, nn in chunks(width, 512):
+    def body(rows, own, other):
+        for n, nn in chunks(max(own, other), 512):
+            nn = min(n + nn, other) - n
             cols = slice(n, n + nn)
-            for m, mm in chunks(rows, 256):
+            for m, mm in chunks(rows, 256) if nn > 0 else ():
                 z = jnp.dot(e_ref[m:m + mm, :], xto_ref[:, cols], preferred_element_type=jnp.float32)
                 t = jnp.tanh(z * (1.0 / SOFT_CAP))
                 g_ref[m:m + mm, tokens + n:tokens + n + nn] = grad_of(
                     t, i * bv + m, lab_ref[1:2, cols], lz_ref[1:2, cols], ts_ref[1:2, cols])
-            own_grads(g_ref, (ta_ref, tb_ref), nt_ref[0], n, nn, rows, i * bv, lab_ref, lz_ref, ts_ref)
-        sides = [(xts_ref[:, :width], g_ref[:rows, :width]), (xto_ref[:, :width], g_ref[:rows, tokens:tokens + width])]
+            nn = min(n + 512, own) - n
+            if nn > 0:
+                own_grads(g_ref, (ta_ref, tb_ref), nt_ref[0], n, nn, rows, i * bv, lab_ref, lz_ref, ts_ref)
+        sides = [(xts_ref[:, :own], g_ref[:rows, :own]), (xto_ref[:, :other], g_ref[:rows, tokens:tokens + other])]
         if rows % 128 == 0:
             (xa, ga), (xb, gb) = sides
             de_ref[:rows, :] = (over_tokens(xa, ga) + over_tokens(xb, gb)).T
@@ -178,11 +188,11 @@
 
     @pl.when(i < nblk - 1)
     def _():
-        per_width(jnp.maximum(nt_ref[0], nt_ref[1]), tokens, functools.partial(body, bv))
+        per_width(nt_ref[0], tokens, lambda own: per_width(nt_ref[1], tokens, functools.partial(body, bv, own)))
 
     @pl.when(i == nblk - 1)
     def _():
-        body(tail, tokens)
+        body(tail, tokens, tokens)
 
 
 def stats_kernel(n_dp, n_tp, vocab, pack_ref, lz_ref, ts_ref, lab_ref, count_ref, loss_ref, got, send_sem, recv_sem):
@@ -272,10 +282,11 @@
         digits = jnp.stack([lab_rows & 63, (lab_rows >> 6) & 63, lab_rows >> 12] + [jnp.zeros_like(lab_rows)] * 5)
         f32, b16 = jnp.float32, jnp.bfloat16
         shape = jax.ShapeDtypeStruct
-        hid_c, xt_own, x32, perm, lab_c = pl.pallas_call(
+        hid_ct, xt_own, x32, perm, lab_c = pl.pallas_call(
             prep_kernel,
-            out_shape=[shape((tokens, dim), b16), shape((dim, tokens), b16), shape((tokens, dim), f32),
+            out_shape=[shape((dim, tokens), b16), shape((dim, tokens), b16), shape((tokens, dim), f32),
                        shape((tokens, tokens), b16), shape((1, tokens), f32)],
+            scratch_shapes=[pltpu.VMEM((tokens, dim), b16)],
             compiler_params=params(),
             name="prep",
         )(hid_rows, mask_rows, digits.astype(b16), gain.reshape(1, dim))
@@ -341,9 +352,9 @@
             pl.CostEstimate(flops=3 * flops, bytes_accessed=elems * 4 + vocab * dim * 6, transcendentals=3 * elems),
         )(nt_both, embed_table, t_a, t_b, xt_own, xt_other, lab, lz, ts_late)
 
-        _, norm_back = jax.vjp(norm_apply, hid_c, gain)
-        grad_rows, grad_gain = norm_back(grad_xt.T)
-        grad_rows = jnp.einsum('it,id->td', perm, grad_rows, preferred_element_type=f32).astype(b16)
+        _, norm_back = jax.vjp(norm_apply_t, hid_ct, gain)
+        grad_cols, grad_gain = norm_back(grad_xt)
+        grad_rows = jnp.einsum('it,di->td', perm, grad_cols, preferred_element_type=f32).astype(b16)
         grad_gain = lax.psum(grad_gain, 'dp')
         return mean_loss, grad_rows.reshape(batch_rows, seq_len, dim), grad_gain, grad_table
 

time: 863 us -> 870 us (level)
  transfers between devices with their start and end apart: 2 -> 2, of which waited for: 1 -> 1; matrix products, arithmetic and copies ran while one was open for 3% -> 3% of each run, Pallas kernels for 32% -> 31%
where the time goes in v5:
time: 870 us; the launch traced here: 863 us
  Pallas kernels  699 us (80%)
  waiting for transfers between devices  114 us (13%)
  between operations  15.2 us (2%)
  other arithmetic  11.2 us (1%)
  matrix products  10.6 us (1%)
    pallas_call x1, Pallas kernels, local_step(): table_call(grad_table_kernel, vocab, bt, [blocks(bt, dim), blocks(bt, edg...  409 us
    pallas_call x1, Pallas kernels, local_step(): table_call(logits_kernel, vocab, bv, [blocks(bv, dim), whole((dim, tokens...  125 us
    pallas_call x1, Pallas kernels, local_step(): table_call(grad_x_kernel, vocab, bx, [blocks(bx, dim), blocks(bx, edge),...  115 us
    psum x1, waiting for transfers between devices, local_step(): grad_xt = lax.psum(gxt, 'tp')  114 us
    pallas_call x1, Pallas kernels, local_step(): pl.pallas_call(functools.partial(stats_kernel, n_dp, n_tp, vocab), out_sh...  30 us
  transfers between devices with their start and end apart: 2, of which 1 were waited for; matrix products, arithmetic and copies ran while one was open for 3% of the time, Pallas kernels for 31%

profile of v5, /device:TPU:0, one launch (start us, length us, event | category | flops | bytes accessed | tf_op | source)
XLA Modules:
  0.0 863.2 jit_solution(16778512751336815555)
XLA Ops:
  7.2 0.7 convert_bitcast_fusion
  7.9 0.6 copy.9
  8.5 0.7 fusion.12
  9.3 1.3 reshape.116.gain_ref
  10.5 0.6 stack.11.dig_ref
  11.2 14.4 %prep.1 = (bf16[896,1536]{1,0:T(8,128)(2,1)}, bf16[896,1536]{1,0:T(8,128)(2,1)}, f32[1536,896]{1,0:T(8,128)}, bf16[1536,1536]{1,0:T(8,128)(2,1)}, f32[1,1536]{1,0:T(1,128)}) custom-call(bf16[1536,896]{1,0:T(8,128)(2,1)} %bitcast.21, f32[1,1536]{1,0:T(1,128)} %bitcast.25, bf16[8,1536]{1,0:T(8,128)(2,1)} %stack.11.dig_ref, f32[1,896]{1,0:T(1,128)} %reshape.116.gain_ref), custom_call_target="tpu_custom_call" | custom-call | tf_op jit(solution)/shard_map/prep/pallas_call | solution.py:285
  25.6 3.3 collective-permute-start
  29.0 1.3 convert_reduce_fusion
  30.9 0.7 subtract_reduce_fusion
  31.7 0.6 broadcast_in_dim.23.lab_ref
  32.3 124.9 %shard_map.84 = (f32[37984,1280]{1,0:T(8,128)}, f32[37984,256]{1,0:T(8,128)}, f32[8,1536]{1,0:T(8,128)}, f32[8,1536]{1,0:T(8,128)}) custom-call(s32[1]{0:T(128)} %bitcast.nt_ref, bf16[37984,896]{1,0:T(8,128)(2,1)} %e_ref.5, bf16[896,1536]{1,0:T(8,128)(2,1)} %get-tuple-element.18.xt_ref.xts_ref, s32[8,1536]{1,0:T(8,128)} %broadcast_in_dim.23.lab_ref), custom_call_target="tpu_custom_call" | custom-call | flops 104551415808 | bytes 301441024 | tf_op jit(solution)/shard_map/pallas_call | solution.py:306
  157.2 0.8 reduce_sum.55
  158.0 0.8 reduce_sum.64
  158.8 0.7 concatenate.3.pack_ref
  159.5 30.0 %stats.1 = (f32[8,1536]{1,0:T(8,128)}, f32[8,1536]{1,0:T(8,128)}, s32[8,1536]{1,0:T(8,128)}, s32[8,128]{1,0:T(8,128)}, f32[8,128]{1,0:T(8,128)}) custom-call(f32[8,1536]{1,0:T(8,128)} %concatenate.3.pack_ref), custom_call_target="tpu_custom_call" | custom-call | tf_op jit(solution)/shard_map/stats/pallas_call | solution.py:317
  189.5 115.0 %shard_map.85 = f32[896,1536]{1,0:T(8,128)} custom-call(s32[1]{0:T(128)} %bitcast.nt_ref, bf16[37984,896]{1,0:T(8,128)(2,1)} %e_ref.5, f32[37984,1280]{1,0:T(8,128)} %get-tuple-element.24.ta_ref, f32[37984,256]{1,0:T(8,128)} %get-tuple-element.25.tb_ref, s32[8,1536]{1,0:T(8,128)} %get-tuple-element.26.lab_ref, f32[8,1536]{1,0:T(8,128)} %get-tuple-element.27.lz_ref, ...), custom_call_target="tpu_custom_call" | custom-call | flops 104551415808 | bytes 301441024 | tf_op jit(solution)/shard_map/pallas_call | solution.py:332
  304.5 1.3 slice.7
  305.9 0.8 add_reduce_fusion
  307.9 113.6 %all-reduce.2.cloned.1.call-done = f32[896,1536]{1,0:T(8,128)} async-done(((f32[896,1536]{1,0:T(8,128)}), f32[896,1536]{1,0:T(8,128)}) %all-reduce.2.cloned.1.call-update) | async-done | bytes 5505040 | tf_op jit(solution)/shard_map/psum | solution.py:338
  421.5 4.1 fusion.4
  425.6 5.5 psum.15
  431.2 10.6 %convolution_convert_fusion = bf16[1536,896]{1,0:T(8,128)(2,1)} fusion(bf16[1536,1536]{1,0:T(8,128)(2,1)} %get-tuple-element.23, bf16[896,1536]{1,0:T(8,128)(2,1)S(1)} %copy-done, f32[896,1536]{1,0:T(8,128)} %all-reduce.2.cloned.1.call-done, f32[1536]{0:T(1024)S(1)} %multiply_multiply_fusion, f32[1536]{0:T(1024)S(1)} %fusion.9, f32[896]{0:T(1024)S(1)} %broadcast_add_fusion), kind=kOutput, calls=%fused_computation.10 | convolution fusion | flops 4238868480 | bytes 15744512 | tf_op jit(solution)/shard_map/it,di->td/dot_general | solution.py:357
  441.7 4.8 prep_other.1.xto_ref
  446.6 409.4 %shard_map.86 = f32[37984,896]{1,0:T(8,128)} custom-call(s32[2]{0:T(128)} %compare_select_fusion.nt_ref, bf16[37984,896]{1,0:T(8,128)(2,1)} %e_ref.5, f32[37984,1280]{1,0:T(8,128)} %get-tuple-element.24.ta_ref, f32[37984,256]{1,0:T(8,128)} %get-tuple-element.25.tb_ref, bf16[896,1536]{1,0:T(8,128)(2,1)} %get-tuple-element.18.xt_ref.xts_ref, ...), custom_call_target="tpu_custom_call" | custom-call | flops 313654247424 | bytes 437575680 | tf_op jit(solution)/shard_map/pallas_call | solution.py:347
  (23 shorter events, 1.4 us)
Async XLA Ops:
  7.2 414.3 %all-reduce.2.cloned.1.call-start = ((), (), s32[]{:S(2)}) async-start(), calls=%async_computation | async-start | bytes 11010048 | tf_op jit(solution)/shard_map/psum | solution.py:338
  25.6 416.1 %collective-permute-start = (f32[1536,896]{1,0:T(8,128)}, f32[1536,896]{1,0:T(8,128)}, u32[]{:S(2)}, u32[]{:S(2)}) collective-permute-start(f32[1536,896]{1,0:T(8,128)} %get-tuple-element.31), channel_id=1, source_target_pairs={{0,4},{4,0},{1,5},{5,1},{2,6},{6,2},{3,7},{7,3}} | collective-permute-start | bytes 16515080 | tf_op jit(solution)/shard_map/ppermute | solution.py:293
  32.3 126.6 %copy-start.1 = (f32[1,1536]{1,0:T(1,128)S(1)}, f32[1,1536]{1,0:T(1,128)}, u32[]{:S(2)}) copy-start(f32[1,1536]{1,0:T(1,128)} %get-tuple-element.19) | copy-start | bytes 18436
  304.5 2.8 copy-start.2
  304.5 2.8 copy-start
Sparse Core Ops, SparseCore 0:
  304.7 116.8 all-reduce.1
